TPU v7x, 32 devices: a whole 2x2x4 slice. The times are simulated.
32 devices in a mesh: gx: 4 (over y, core), gy: 2 (over x), gz: 4 (over z).
Axes of the slice: x: 2, y: 2, z: 4, core: 2. Of those that a mesh axis runs over, the one named last changes fastest.
Arguments:
- pressure_now: float32 [64, 64, 512], P('gx', 'gy', 'gz'), may hold values from -6 to 6
- pressure_before: float32 [64, 64, 512], P('gx', 'gy', 'gz'), may hold values from -6 to 6
- region_code: int32 [64, 64, 512], P('gx', 'gy', 'gz'), may hold values from 0 to 7
- velocity: float32 [8], replicated, may hold values from 0.2 to 0.42
- wavelet: float32 [6, 16], replicated, may hold values from -6 to 6
- source_cell: int32 [16], replicated, may hold values from 0 to 2097151
Outputs:
- pressure: float32 [64, 64, 512], P('gx', 'gy', 'gz')
- previous: float32 [64, 64, 512], P('gx', 'gy', 'gz')
Inputs may be any that keep to these rules, and one draw needn't show every extreme that they name: source_cell[s] is the flat index x * 64 * 512 + y * 512 + z of a grid cell; sources may share a cell.
All inputs are finite; a program needn't handle non-finite values.
Results may differ from a plain program's by a relative error of at most 0.00002.
Values sent between devices are 32-bit elements; how exact they have to be, the bound alone decides.
A program may use at most 64 MiB of HBM per device.

v0:
```python
import jax
import jax.numpy as jnp
from jax import lax
from jax.sharding import PartitionSpec as P

STEPS = 6


CENTRE = -205.0 / 72.0
WEIGHTS = (8.0 / 5.0, -1.0 / 5.0, 8.0 / 315.0, -1.0 / 560.0)


def padded(block, sides, width, periodic):
    for axis, dim in sides:
        count = lax.axis_size(axis)
        forward = [(i, i + 1) for i in range(count - 1)]
        if periodic:
            forward.append((count - 1, 0))
        backward = [(target, source) for source, target in forward]
        low = lax.ppermute(
            lax.slice_in_dim(block, block.shape[dim] - width, None, axis=dim), axis, forward
        )
        high = lax.ppermute(lax.slice_in_dim(block, 0, width, axis=dim), axis, backward)
        block = jnp.concatenate([low, block, high], axis=dim)
    return block


def cut(field, start, size):
    return lax.slice(field, tuple(start), tuple((a + b for a, b in zip(start, size))))


def along(field, axis, start, size):
    total = None
    for step_k, weight in enumerate(WEIGHTS, 1):
        upper = list(start)
        upper[axis] = upper[axis] + step_k
        lower = list(start)
        lower[axis] = lower[axis] - step_k
        term = weight * (cut(field, upper, size) + cut(field, lower, size))
        total = term if total is None else total + term
    return total


def rates(codes, velocity):
    speed = jnp.zeros(codes.shape, jnp.float32)
    for region in range(velocity.shape[0]):
        speed = jnp.where(codes == region, velocity[region], speed)
    return speed * speed


def per_device(pressure_now, pressure_before, region_code, velocity, wavelet, source_cell):
    size = pressure_now.shape
    count_x, count_y, count_z = size
    grid_x = count_x * lax.axis_size("gx")
    grid_y = count_y * lax.axis_size("gy")
    grid_z = count_z * lax.axis_size("gz")
    first_x = lax.axis_index("gx") * count_x
    first_y = lax.axis_index("gy") * count_y
    first_z = lax.axis_index("gz") * count_z
    source_x = source_cell // (grid_y * grid_z)
    source_y = source_cell // grid_z % grid_y
    source_z = source_cell % grid_z
    current = pressure_now
    before = pressure_before
    rate = rates(region_code, velocity)
    for step in range(STEPS):
        wide_x = padded(current, (("gx", 0),), 4, True)
        wide_yz = padded(current, (("gy", 1), ("gz", 2)), 4, False)
        laplace = (
            3.0 * CENTRE * current
            + along(wide_x, 0, (4, 0, 0), size)
            + along(wide_yz, 1, (0, 4, 4), size)
            + along(wide_yz, 2, (0, 4, 4), size)
        )
        following = 2.0 * current - before + rate * laplace
        local_x = (source_x - first_x) % grid_x
        local_y = source_y - first_y
        local_z = source_z - first_z
        inside_box = (
            (local_x < size[0])
            & (local_y >= 0)
            & (local_y < size[1])
            & (local_z >= 0)
            & (local_z < size[2])
        )
        cells = size[0] * size[1] * size[2]
        flat = jnp.where(inside_box, (local_x * size[1] + local_y) * size[2] + local_z, cells)
        following = following.reshape(-1).at[flat].add(wavelet[step], mode="drop").reshape(size)
        before = current
        current = following
    return (current, before)


def solution(mesh):
    placed = (P("gx", "gy", "gz"), P("gx", "gy", "gz"), P("gx", "gy", "gz"), P(), P(), P())
    return jax.shard_map(
        per_device,
        mesh=mesh,
        in_specs=placed,
        out_specs=(P("gx", "gy", "gz"), P("gx", "gy", "gz")),
        check_vma=False,
    )
```

profile of v0, /device:TPU:0, one launch (start us, length us, event | category | flops | bytes accessed | tf_op | source)
XLA Modules:
  0.0 166.9 jit_solution(10241812409695056651)
XLA Ops:
  1.6 4.9 %collective-permute-start.3 = (f32[16,4,128]{2,1,0:T(4,128)S(1)}, f32[16,4,128]{2,1,0:T(4,128)S(1)}, u32[]{:S(2)}, u32[]{:S(2)}) collective-permute-start(f32[16,4,128]{2,1,0:T(4,128)S(1)} %get-tuple-element.52), channel_id=1, source_target_pairs={{0,4},{1,5},{2,6},{3,7},{8,12},{9,13},{10,14},{11,15},{16,20},{17,... | collective-permute-start | bytes 98312 | tf_op jit(solution)/shard_map/ppermute | solution.py:20
  6.5 1.3 collective-permute-start.2
  8.7 1.7 %collective-permute-start = (f32[4,32,128]{2,1,0:T(8,128)S(1)}, f32[4,32,128]{2,1,0:T(8,128)S(1)}, u32[]{:S(2)}, u32[]{:S(2)}) collective-permute-start(f32[4,32,128]{2,1,0:T(8,128)S(1)} %get-tuple-element.46), channel_id=1, source_target_pairs={{8,0},{16,8},{24,16},{0,24},{9,1},{17,9},{25,17},{1,25},{10,2},{18... | collective-permute-start | bytes 196616 | tf_op jit(solution)/shard_map/ppermute | solution.py:23
  12.5 1.3 collective-permute-start.4
  13.8 4.6 %collective-permute-start.5 = (f32[16,40,4]{2,1,0:T(8,128)S(1)}, f32[16,40,4]{2,1,0:T(8,128)S(1)}, u32[]{:S(2)}, u32[]{:S(2)}) collective-permute-start(f32[16,40,4]{2,1,0:T(8,128)S(1)} %get-tuple-element.25), channel_id=1, source_target_pairs={{0,1},{1,2},{2,3},{4,5},{5,6},{6,7},{8,9},{9,10},{10,11},{12,13},{... | collective-permute-start | bytes 30728 | tf_op jit(solution)/shard_map/ppermute | solution.py:20
  19.0 4.4 %collective-permute-done.4 = f32[16,40,4]{2,1,0:T(8,128)S(1)} collective-permute-done((f32[16,40,4]{2,1,0:T(8,128)S(1)}, f32[16,40,4]{2,1,0:T(8,128)S(1)}, u32[]{:S(2)}, u32[]{:S(2)}) %collective-permute-start.4) | collective-permute-done | bytes 10272 | tf_op jit(solution)/shard_map/ppermute | solution.py:23
  26.0 5.9 %fusion.183 = f32[16,32,128]{2,1,0:T(8,128)S(1)} fusion(f32[16,32,128]{2,1,0:T(8,128)S(1)} %copy-done.2, f32[16,4,128]{2,1,0:T(4,128)S(1)} %collective-permute-done.3, f32[16,40,132]{2,1,0:T(8,128)S(1)} %get-tuple-element.23, f32[16,40,132]{2,1,0:T(8,128)S(1)} %get-tuple-element.22, f32[16,36,128]{2,1,0:T(8,128)S(1)} %constant_dynamic-update-slice_fusion.4, ...), kind=kLoop, calls=%fused_computation.333 | loop fusion | flops 4063232 | bytes 6324256 | tf_op jit(solution)/shard_map/add | solution.py:75
  32.8 4.5 %collective-permute-start.9 = (f32[16,4,128]{2,1,0:T(4,128)S(1)}, f32[16,4,128]{2,1,0:T(4,128)S(1)}, u32[]{:S(2)}, u32[]{:S(2)}) collective-permute-start(f32[16,4,128]{2,1,0:T(4,128)S(1)} %get-tuple-element.43), channel_id=1, source_target_pairs={{0,4},{1,5},{2,6},{3,7},{8,12},{9,13},{10,14},{11,15},{16,20},{17,... | collective-permute-start | bytes 98312 | tf_op jit(solution)/shard_map/ppermute | solution.py:20
  37.3 1.3 collective-permute-start.8
  38.9 4.2 %collective-permute-done.8 = f32[16,4,128]{2,1,0:T(4,128)S(1)} collective-permute-done((f32[16,4,128]{2,1,0:T(4,128)S(1)}, f32[16,4,128]{2,1,0:T(4,128)S(1)}, u32[]{:S(2)}, u32[]{:S(2)}) %collective-permute-start.8) | collective-permute-done | bytes 32800 | tf_op jit(solution)/shard_map/ppermute | solution.py:23
  43.3 1.3 collective-permute-start.10
  44.6 5.0 %collective-permute-start.11 = (f32[16,40,4]{2,1,0:T(8,128)S(1)}, f32[16,40,4]{2,1,0:T(8,128)S(1)}, u32[]{:S(2)}, u32[]{:S(2)}) collective-permute-start(f32[16,40,4]{2,1,0:T(8,128)S(1)} %get-tuple-element.21), channel_id=1, source_target_pairs={{0,1},{1,2},{2,3},{4,5},{5,6},{6,7},{8,9},{9,10},{10,11},{12,13},{... | collective-permute-start | bytes 30728 | tf_op jit(solution)/shard_map/ppermute | solution.py:20
  49.8 1.7 %collective-permute-start.6 = (f32[4,32,128]{2,1,0:T(8,128)S(1)}, f32[4,32,128]{2,1,0:T(8,128)S(1)}, u32[]{:S(2)}, u32[]{:S(2)}) collective-permute-start(f32[4,32,128]{2,1,0:T(8,128)S(1)} %bitcast.74), channel_id=1, source_target_pairs={{8,0},{16,8},{24,16},{0,24},{9,1},{17,9},{25,17},{1,25},{10,2},{18... | collective-permute-start | bytes 196616 | tf_op jit(solution)/shard_map/ppermute | solution.py:23
  51.5 1.4 collective-permute-done.10
  52.9 1.3 collective-permute-done.11
  54.6 5.9 %fusion.148 = f32[16,32,128]{2,1,0:T(8,128)S(1)} fusion(f32[16,32,128]{2,1,0:T(8,128)S(1)} %bitcast.58, f32[4,32,128]{2,1,0:T(8,128)S(1)} %collective-permute-done.7, f32[4,32,128]{2,1,0:T(8,128)S(1)} %collective-permute-done.6, f32[16,4,128]{2,1,0:T(4,128)S(1)} %collective-permute-done.9, f32[16,4,128]{2,1,0:T(4,128)S(1)} %collective-permute-done.8, ...), kind=kLoop, calls=%fused_computation.298 | loop fusion | flops 4849664 | bytes 3342368 | tf_op jit(solution)/shard_map/add | solution.py:75
  61.3 1.8 %collective-permute-start.15 = (f32[16,4,128]{2,1,0:T(4,128)S(1)}, f32[16,4,128]{2,1,0:T(4,128)S(1)}, u32[]{:S(2)}, u32[]{:S(2)}) collective-permute-start(f32[16,4,128]{2,1,0:T(4,128)S(1)} %get-tuple-element.39), channel_id=1, source_target_pairs={{0,4},{1,5},{2,6},{3,7},{8,12},{9,13},{10,14},{11,15},{16,20},{17,... | collective-permute-start | bytes 98312 | tf_op jit(solution)/shard_map/ppermute | solution.py:20
  63.1 1.3 collective-permute-start.14
  64.7 4.2 %collective-permute-done.14 = f32[16,4,128]{2,1,0:T(4,128)S(1)} collective-permute-done((f32[16,4,128]{2,1,0:T(4,128)S(1)}, f32[16,4,128]{2,1,0:T(4,128)S(1)}, u32[]{:S(2)}, u32[]{:S(2)}) %collective-permute-start.14) | collective-permute-done | bytes 32800 | tf_op jit(solution)/shard_map/ppermute | solution.py:23
  69.1 1.3 collective-permute-start.16
  70.4 5.0 %collective-permute-start.17 = (f32[16,40,4]{2,1,0:T(8,128)S(1)}, f32[16,40,4]{2,1,0:T(8,128)S(1)}, u32[]{:S(2)}, u32[]{:S(2)}) collective-permute-start(f32[16,40,4]{2,1,0:T(8,128)S(1)} %get-tuple-element.17), channel_id=1, source_target_pairs={{0,1},{1,2},{2,3},{4,5},{5,6},{6,7},{8,9},{9,10},{10,11},{12,13},{... | collective-permute-start | bytes 30728 | tf_op jit(solution)/shard_map/ppermute | solution.py:20
  75.6 1.7 %collective-permute-start.12 = (f32[4,32,128]{2,1,0:T(8,128)S(1)}, f32[4,32,128]{2,1,0:T(8,128)S(1)}, u32[]{:S(2)}, u32[]{:S(2)}) collective-permute-start(f32[4,32,128]{2,1,0:T(8,128)S(1)} %bitcast.75), channel_id=1, source_target_pairs={{8,0},{16,8},{24,16},{0,24},{9,1},{17,9},{25,17},{1,25},{10,2},{18... | collective-permute-start | bytes 196616 | tf_op jit(solution)/shard_map/ppermute | solution.py:23
  77.3 1.8 %collective-permute-done.16 = f32[16,40,4]{2,1,0:T(8,128)S(1)} collective-permute-done((f32[16,40,4]{2,1,0:T(8,128)S(1)}, f32[16,40,4]{2,1,0:T(8,128)S(1)}, u32[]{:S(2)}, u32[]{:S(2)}) %collective-permute-start.16) | collective-permute-done | bytes 10272 | tf_op jit(solution)/shard_map/ppermute | solution.py:23
  80.6 5.9 %fusion.113 = f32[16,32,128]{2,1,0:T(8,128)S(1)} fusion(f32[16,32,128]{2,1,0:T(8,128)S(1)} %bitcast.64, f32[4,32,128]{2,1,0:T(8,128)S(1)} %collective-permute-done.13, f32[4,32,128]{2,1,0:T(8,128)S(1)} %collective-permute-done.12, f32[16,4,128]{2,1,0:T(4,128)S(1)} %collective-permute-done.15, f32[16,4,128]{2,1,0:T(4,128)S(1)} %collective-permute-done.14, ...), kind=kLoop, calls=%fused_computation.263 | loop fusion | flops 4849664 | bytes 3342368 | tf_op jit(solution)/shard_map/add | solution.py:75
  87.4 1.9 %collective-permute-start.21 = (f32[16,4,128]{2,1,0:T(4,128)S(1)}, f32[16,4,128]{2,1,0:T(4,128)S(1)}, u32[]{:S(2)}, u32[]{:S(2)}) collective-permute-start(f32[16,4,128]{2,1,0:T(4,128)S(1)} %get-tuple-element.35), channel_id=1, source_target_pairs={{0,4},{1,5},{2,6},{3,7},{8,12},{9,13},{10,14},{11,15},{16,20},{17,... | collective-permute-start | bytes 98312 | tf_op jit(solution)/shard_map/ppermute | solution.py:20
  89.3 1.3 collective-permute-start.20
  90.9 4.2 %collective-permute-done.20 = f32[16,4,128]{2,1,0:T(4,128)S(1)} collective-permute-done((f32[16,4,128]{2,1,0:T(4,128)S(1)}, f32[16,4,128]{2,1,0:T(4,128)S(1)}, u32[]{:S(2)}, u32[]{:S(2)}) %collective-permute-start.20) | collective-permute-done | bytes 32800 | tf_op jit(solution)/shard_map/ppermute | solution.py:23
  95.3 1.3 collective-permute-start.22
  96.6 5.0 %collective-permute-start.23 = (f32[16,40,4]{2,1,0:T(8,128)S(1)}, f32[16,40,4]{2,1,0:T(8,128)S(1)}, u32[]{:S(2)}, u32[]{:S(2)}) collective-permute-start(f32[16,40,4]{2,1,0:T(8,128)S(1)} %get-tuple-element.13), channel_id=1, source_target_pairs={{0,1},{1,2},{2,3},{4,5},{5,6},{6,7},{8,9},{9,10},{10,11},{12,13},{... | collective-permute-start | bytes 30728 | tf_op jit(solution)/shard_map/ppermute | solution.py:20
  101.8 1.7 %collective-permute-start.18 = (f32[4,32,128]{2,1,0:T(8,128)S(1)}, f32[4,32,128]{2,1,0:T(8,128)S(1)}, u32[]{:S(2)}, u32[]{:S(2)}) collective-permute-start(f32[4,32,128]{2,1,0:T(8,128)S(1)} %bitcast.76), channel_id=1, source_target_pairs={{8,0},{16,8},{24,16},{0,24},{9,1},{17,9},{25,17},{1,25},{10,2},{18... | collective-permute-start | bytes 196616 | tf_op jit(solution)/shard_map/ppermute | solution.py:23
  103.5 1.3 collective-permute-done.22
  104.8 1.4 collective-permute-done.23
  106.6 5.9 %fusion.78 = f32[16,32,128]{2,1,0:T(8,128)S(1)} fusion(f32[16,32,128]{2,1,0:T(8,128)S(1)} %bitcast.46, f32[4,32,128]{2,1,0:T(8,128)S(1)} %collective-permute-done.19, f32[4,32,128]{2,1,0:T(8,128)S(1)} %collective-permute-done.18, f32[16,4,128]{2,1,0:T(4,128)S(1)} %collective-permute-done.21, f32[16,4,128]{2,1,0:T(4,128)S(1)} %collective-permute-done.20, ...), kind=kLoop, calls=%fused_computation.228 | loop fusion | flops 4849664 | bytes 3342368 | tf_op jit(solution)/shard_map/add | solution.py:75
  113.3 1.7 %collective-permute-start.27 = (f32[16,4,128]{2,1,0:T(4,128)S(1)}, f32[16,4,128]{2,1,0:T(4,128)S(1)}, u32[]{:S(2)}, u32[]{:S(2)}) collective-permute-start(f32[16,4,128]{2,1,0:T(4,128)S(1)} %get-tuple-element.31), channel_id=1, source_target_pairs={{0,4},{1,5},{2,6},{3,7},{8,12},{9,13},{10,14},{11,15},{16,20},{17,... | collective-permute-start | bytes 98312 | tf_op jit(solution)/shard_map/ppermute | solution.py:20
  115.0 1.3 collective-permute-start.26
  116.6 4.2 %collective-permute-done.26 = f32[16,4,128]{2,1,0:T(4,128)S(1)} collective-permute-done((f32[16,4,128]{2,1,0:T(4,128)S(1)}, f32[16,4,128]{2,1,0:T(4,128)S(1)}, u32[]{:S(2)}, u32[]{:S(2)}) %collective-permute-start.26) | collective-permute-done | bytes 32800 | tf_op jit(solution)/shard_map/ppermute | solution.py:23
  121.0 1.3 collective-permute-start.28
  122.3 5.0 %collective-permute-start.29 = (f32[16,40,4]{2,1,0:T(8,128)S(1)}, f32[16,40,4]{2,1,0:T(8,128)S(1)}, u32[]{:S(2)}, u32[]{:S(2)}) collective-permute-start(f32[16,40,4]{2,1,0:T(8,128)S(1)} %get-tuple-element.9), channel_id=1, source_target_pairs={{0,1},{1,2},{2,3},{4,5},{5,6},{6,7},{8,9},{9,10},{10,11},{12,13},{... | collective-permute-start | bytes 30728 | tf_op jit(solution)/shard_map/ppermute | solution.py:20
  127.5 1.7 %collective-permute-start.24 = (f32[4,32,128]{2,1,0:T(8,128)S(1)}, f32[4,32,128]{2,1,0:T(8,128)S(1)}, u32[]{:S(2)}, u32[]{:S(2)}) collective-permute-start(f32[4,32,128]{2,1,0:T(8,128)S(1)} %bitcast.77), channel_id=1, source_target_pairs={{8,0},{16,8},{24,16},{0,24},{9,1},{17,9},{25,17},{1,25},{10,2},{18... | collective-permute-start | bytes 196616 | tf_op jit(solution)/shard_map/ppermute | solution.py:23
  129.2 2.4 %collective-permute-done.28 = f32[16,40,4]{2,1,0:T(8,128)S(1)} collective-permute-done((f32[16,40,4]{2,1,0:T(8,128)S(1)}, f32[16,40,4]{2,1,0:T(8,128)S(1)}, u32[]{:S(2)}, u32[]{:S(2)}) %collective-permute-start.28) | collective-permute-done | bytes 10272 | tf_op jit(solution)/shard_map/ppermute | solution.py:23
  133.2 5.9 %fusion.43 = f32[16,32,128]{2,1,0:T(8,128)S(1)} fusion(f32[16,32,128]{2,1,0:T(8,128)S(1)} %bitcast.52, f32[4,32,128]{2,1,0:T(8,128)S(1)} %collective-permute-done.25, f32[4,32,128]{2,1,0:T(8,128)S(1)} %collective-permute-done.24, f32[16,4,128]{2,1,0:T(4,128)S(1)} %collective-permute-done.27, f32[16,4,128]{2,1,0:T(4,128)S(1)} %collective-permute-done.26, ...), kind=kLoop, calls=%fused_computation.193 | loop fusion | flops 4849664 | bytes 3342368 | tf_op jit(solution)/shard_map/add | solution.py:75
  140.0 1.9 %collective-permute-start.33 = (f32[16,4,128]{2,1,0:T(4,128)S(1)}, f32[16,4,128]{2,1,0:T(4,128)S(1)}, u32[]{:S(2)}, u32[]{:S(2)}) collective-permute-start(f32[16,4,128]{2,1,0:T(4,128)S(1)} %get-tuple-element.27), channel_id=1, source_target_pairs={{0,4},{1,5},{2,6},{3,7},{8,12},{9,13},{10,14},{11,15},{16,20},{17,... | collective-permute-start | bytes 98312 | tf_op jit(solution)/shard_map/ppermute | solution.py:20
  141.9 1.3 collective-permute-start.32
  143.5 4.2 %collective-permute-done.32 = f32[16,4,128]{2,1,0:T(4,128)S(1)} collective-permute-done((f32[16,4,128]{2,1,0:T(4,128)S(1)}, f32[16,4,128]{2,1,0:T(4,128)S(1)}, u32[]{:S(2)}, u32[]{:S(2)}) %collective-permute-start.32) | collective-permute-done | bytes 32800 | tf_op jit(solution)/shard_map/ppermute | solution.py:23
  149.2 5.0 %collective-permute-start.35 = (f32[16,40,4]{2,1,0:T(8,128)S(1)}, f32[16,40,4]{2,1,0:T(8,128)S(1)}, u32[]{:S(2)}, u32[]{:S(2)}) collective-permute-start(f32[16,40,4]{2,1,0:T(8,128)S(1)} %get-tuple-element.5), channel_id=1, source_target_pairs={{0,1},{1,2},{2,3},{4,5},{5,6},{6,7},{8,9},{9,10},{10,11},{12,13},{... | collective-permute-start | bytes 30728 | tf_op jit(solution)/shard_map/ppermute | solution.py:20
  154.3 1.7 %collective-permute-start.30 = (f32[4,32,128]{2,1,0:T(8,128)S(1)}, f32[4,32,128]{2,1,0:T(8,128)S(1)}, u32[]{:S(2)}, u32[]{:S(2)}) collective-permute-start(f32[4,32,128]{2,1,0:T(8,128)S(1)} %bitcast.78), channel_id=1, source_target_pairs={{8,0},{16,8},{24,16},{0,24},{9,1},{17,9},{25,17},{1,25},{10,2},{18... | collective-permute-start | bytes 196616 | tf_op jit(solution)/shard_map/ppermute | solution.py:23
  156.1 1.9 %collective-permute-done.34 = f32[16,40,4]{2,1,0:T(8,128)S(1)} collective-permute-done((f32[16,40,4]{2,1,0:T(8,128)S(1)}, f32[16,40,4]{2,1,0:T(8,128)S(1)}, u32[]{:S(2)}, u32[]{:S(2)}) %collective-permute-start.34) | collective-permute-done | bytes 10272 | tf_op jit(solution)/shard_map/ppermute | solution.py:23
  159.5 5.9 %fusion.8 = f32[16,32,128]{2,1,0:T(8,128)S(1)} fusion(f32[16,32,128]{2,1,0:T(8,128)S(1)} %bitcast.70, f32[4,32,128]{2,1,0:T(8,128)S(1)} %collective-permute-done.31, f32[4,32,128]{2,1,0:T(8,128)S(1)} %collective-permute-done.30, f32[16,4,128]{2,1,0:T(4,128)S(1)} %collective-permute-done.33, f32[16,4,128]{2,1,0:T(4,128)S(1)} %collective-permute-done.32, ...), kind=kLoop, calls=%fused_computation.158 | loop fusion | flops 4849664 | bytes 3342368 | tf_op jit(solution)/shard_map/add | solution.py:75
  (89 shorter events, 21.8 us)
Async XLA Ops:
  0.6 11.6 %copy-start.2 = (f32[16,32,128]{2,1,0:T(8,128)S(1)}, f32[16,32,128]{2,1,0:T(8,128)}, u32[]{:S(2)}) copy-start(f32[16,32,128]{2,1,0:T(8,128)} %param.6) | copy-start | bytes 786436
  1.6 10.2 %collective-permute-start.3 = (f32[16,4,128]{2,1,0:T(4,128)S(1)}, f32[16,4,128]{2,1,0:T(4,128)S(1)}, u32[]{:S(2)}, u32[]{:S(2)}) collective-permute-start(f32[16,4,128]{2,1,0:T(4,128)S(1)} %get-tuple-element.52), channel_id=1, source_target_pairs={{0,4},{1,5},{2,6},{3,7},{8,12},{9,13},{10,14},{11,15},{16,20},{17,... | collective-permute-start | bytes 98312 | tf_op jit(solution)/shard_map/ppermute | solution.py:20
  6.5 5.8 %collective-permute-start.2 = (f32[16,4,128]{2,1,0:T(4,128)S(1)}, f32[16,4,128]{2,1,0:T(4,128)S(1)}, u32[]{:S(2)}, u32[]{:S(2)}) collective-permute-start(f32[16,4,128]{2,1,0:T(4,128)S(1)} %get-tuple-element.51), channel_id=1, source_target_pairs={{4,0},{5,1},{6,2},{7,3},{12,8},{13,9},{14,10},{15,11},{20,16},{21,... | collective-permute-start | bytes 98312 | tf_op jit(solution)/shard_map/ppermute | solution.py:23
  8.6 16.3 %collective-permute-start.1 = (f32[4,32,128]{2,1,0:T(8,128)S(1)}, f32[4,32,128]{2,1,0:T(8,128)S(1)}, u32[]{:S(2)}, u32[]{:S(2)}) collective-permute-start(f32[4,32,128]{2,1,0:T(8,128)S(1)} %get-tuple-element.47), channel_id=1, source_target_pairs={{0,8},{8,16},{16,24},{24,0},{1,9},{9,17},{17,25},{25,1},{2,10},{10... | collective-permute-start | bytes 196616 | tf_op jit(solution)/shard_map/ppermute | solution.py:20
  8.7 16.4 %collective-permute-start = (f32[4,32,128]{2,1,0:T(8,128)S(1)}, f32[4,32,128]{2,1,0:T(8,128)S(1)}, u32[]{:S(2)}, u32[]{:S(2)}) collective-permute-start(f32[4,32,128]{2,1,0:T(8,128)S(1)} %get-tuple-element.46), channel_id=1, source_target_pairs={{8,0},{16,8},{24,16},{0,24},{9,1},{17,9},{25,17},{1,25},{10,2},{18... | collective-permute-start | bytes 196616 | tf_op jit(solution)/shard_map/ppermute | solution.py:23
  10.4 0.7 copy-start.6
  11.1 0.7 copy-start.7
  12.5 5.9 %copy-start.5 = (f32[8]{0:T(128)S(1)}, f32[8]{0:T(128)}, u32[]{:S(2)}) copy-start(f32[8]{0:T(128)} %param.9) | copy-start | bytes 100
  12.5 11.0 %collective-permute-start.4 = (f32[16,40,4]{2,1,0:T(8,128)S(1)}, f32[16,40,4]{2,1,0:T(8,128)S(1)}, u32[]{:S(2)}, u32[]{:S(2)}) collective-permute-start(f32[16,40,4]{2,1,0:T(8,128)S(1)} %get-tuple-element.24), channel_id=1, source_target_pairs={{1,0},{2,1},{3,2},{5,4},{6,5},{7,6},{9,8},{10,9},{11,10},{13,12},{... | collective-permute-start | bytes 30728 | tf_op jit(solution)/shard_map/ppermute | solution.py:23
  13.8 10.9 %collective-permute-start.5 = (f32[16,40,4]{2,1,0:T(8,128)S(1)}, f32[16,40,4]{2,1,0:T(8,128)S(1)}, u32[]{:S(2)}, u32[]{:S(2)}) collective-permute-start(f32[16,40,4]{2,1,0:T(8,128)S(1)} %get-tuple-element.25), channel_id=1, source_target_pairs={{0,1},{1,2},{2,3},{4,5},{5,6},{6,7},{8,9},{9,10},{10,11},{12,13},{... | collective-permute-start | bytes 30728 | tf_op jit(solution)/shard_map/ppermute | solution.py:20
  25.0 1.0 copy-start.1
  25.0 1.0 copy-start.4
  32.8 6.1 %collective-permute-start.9 = (f32[16,4,128]{2,1,0:T(4,128)S(1)}, f32[16,4,128]{2,1,0:T(4,128)S(1)}, u32[]{:S(2)}, u32[]{:S(2)}) collective-permute-start(f32[16,4,128]{2,1,0:T(4,128)S(1)} %get-tuple-element.43), channel_id=1, source_target_pairs={{0,4},{1,5},{2,6},{3,7},{8,12},{9,13},{10,14},{11,15},{16,20},{17,... | collective-permute-start | bytes 98312 | tf_op jit(solution)/shard_map/ppermute | solution.py:20
  37.3 5.8 %collective-permute-start.8 = (f32[16,4,128]{2,1,0:T(4,128)S(1)}, f32[16,4,128]{2,1,0:T(4,128)S(1)}, u32[]{:S(2)}, u32[]{:S(2)}) collective-permute-start(f32[16,4,128]{2,1,0:T(4,128)S(1)} %get-tuple-element.42), channel_id=1, source_target_pairs={{4,0},{5,1},{6,2},{7,3},{12,8},{13,9},{14,10},{15,11},{20,16},{21,... | collective-permute-start | bytes 98312 | tf_op jit(solution)/shard_map/ppermute | solution.py:23
  43.3 9.6 %collective-permute-start.10 = (f32[16,40,4]{2,1,0:T(8,128)S(1)}, f32[16,40,4]{2,1,0:T(8,128)S(1)}, u32[]{:S(2)}, u32[]{:S(2)}) collective-permute-start(f32[16,40,4]{2,1,0:T(8,128)S(1)} %get-tuple-element.20), channel_id=1, source_target_pairs={{1,0},{2,1},{3,2},{5,4},{6,5},{7,6},{9,8},{10,9},{11,10},{13,12},{... | collective-permute-start | bytes 30728 | tf_op jit(solution)/shard_map/ppermute | solution.py:23
  44.6 9.6 %collective-permute-start.11 = (f32[16,40,4]{2,1,0:T(8,128)S(1)}, f32[16,40,4]{2,1,0:T(8,128)S(1)}, u32[]{:S(2)}, u32[]{:S(2)}) collective-permute-start(f32[16,40,4]{2,1,0:T(8,128)S(1)} %get-tuple-element.21), channel_id=1, source_target_pairs={{0,1},{1,2},{2,3},{4,5},{5,6},{6,7},{8,9},{9,10},{10,11},{12,13},{... | collective-permute-start | bytes 30728 | tf_op jit(solution)/shard_map/ppermute | solution.py:20
  49.7 4.9 %collective-permute-start.7 = (f32[4,32,128]{2,1,0:T(8,128)S(1)}, f32[4,32,128]{2,1,0:T(8,128)S(1)}, u32[]{:S(2)}, u32[]{:S(2)}) collective-permute-start(f32[4,32,128]{2,1,0:T(8,128)S(1)} %bitcast.79), channel_id=1, source_target_pairs={{0,8},{8,16},{16,24},{24,0},{1,9},{9,17},{17,25},{25,1},{2,10},{10... | collective-permute-start | bytes 196616 | tf_op jit(solution)/shard_map/ppermute | solution.py:20
  49.8 4.8 %collective-permute-start.6 = (f32[4,32,128]{2,1,0:T(8,128)S(1)}, f32[4,32,128]{2,1,0:T(8,128)S(1)}, u32[]{:S(2)}, u32[]{:S(2)}) collective-permute-start(f32[4,32,128]{2,1,0:T(8,128)S(1)} %bitcast.74), channel_id=1, source_target_pairs={{8,0},{16,8},{24,16},{0,24},{9,1},{17,9},{25,17},{1,25},{10,2},{18... | collective-permute-start | bytes 196616 | tf_op jit(solution)/shard_map/ppermute | solution.py:23
  61.3 3.4 %collective-permute-start.15 = (f32[16,4,128]{2,1,0:T(4,128)S(1)}, f32[16,4,128]{2,1,0:T(4,128)S(1)}, u32[]{:S(2)}, u32[]{:S(2)}) collective-permute-start(f32[16,4,128]{2,1,0:T(4,128)S(1)} %get-tuple-element.39), channel_id=1, source_target_pairs={{0,4},{1,5},{2,6},{3,7},{8,12},{9,13},{10,14},{11,15},{16,20},{17,... | collective-permute-start | bytes 98312 | tf_op jit(solution)/shard_map/ppermute | solution.py:20
  63.1 5.8 %collective-permute-start.14 = (f32[16,4,128]{2,1,0:T(4,128)S(1)}, f32[16,4,128]{2,1,0:T(4,128)S(1)}, u32[]{:S(2)}, u32[]{:S(2)}) collective-permute-start(f32[16,4,128]{2,1,0:T(4,128)S(1)} %get-tuple-element.38), channel_id=1, source_target_pairs={{4,0},{5,1},{6,2},{7,3},{12,8},{13,9},{14,10},{15,11},{20,16},{21,... | collective-permute-start | bytes 98312 | tf_op jit(solution)/shard_map/ppermute | solution.py:23
  69.1 10.0 %collective-permute-start.16 = (f32[16,40,4]{2,1,0:T(8,128)S(1)}, f32[16,40,4]{2,1,0:T(8,128)S(1)}, u32[]{:S(2)}, u32[]{:S(2)}) collective-permute-start(f32[16,40,4]{2,1,0:T(8,128)S(1)} %get-tuple-element.16), channel_id=1, source_target_pairs={{1,0},{2,1},{3,2},{5,4},{6,5},{7,6},{9,8},{10,9},{11,10},{13,12},{... | collective-permute-start | bytes 30728 | tf_op jit(solution)/shard_map/ppermute | solution.py:23
  70.4 9.8 %collective-permute-start.17 = (f32[16,40,4]{2,1,0:T(8,128)S(1)}, f32[16,40,4]{2,1,0:T(8,128)S(1)}, u32[]{:S(2)}, u32[]{:S(2)}) collective-permute-start(f32[16,40,4]{2,1,0:T(8,128)S(1)} %get-tuple-element.17), channel_id=1, source_target_pairs={{0,1},{1,2},{2,3},{4,5},{5,6},{6,7},{8,9},{9,10},{10,11},{12,13},{... | collective-permute-start | bytes 30728 | tf_op jit(solution)/shard_map/ppermute | solution.py:20
  75.5 5.1 %collective-permute-start.13 = (f32[4,32,128]{2,1,0:T(8,128)S(1)}, f32[4,32,128]{2,1,0:T(8,128)S(1)}, u32[]{:S(2)}, u32[]{:S(2)}) collective-permute-start(f32[4,32,128]{2,1,0:T(8,128)S(1)} %bitcast.80), channel_id=1, source_target_pairs={{0,8},{8,16},{16,24},{24,0},{1,9},{9,17},{17,25},{25,1},{2,10},{10... | collective-permute-start | bytes 196616 | tf_op jit(solution)/shard_map/ppermute | solution.py:20
  75.6 5.1 %collective-permute-start.12 = (f32[4,32,128]{2,1,0:T(8,128)S(1)}, f32[4,32,128]{2,1,0:T(8,128)S(1)}, u32[]{:S(2)}, u32[]{:S(2)}) collective-permute-start(f32[4,32,128]{2,1,0:T(8,128)S(1)} %bitcast.75), channel_id=1, source_target_pairs={{8,0},{16,8},{24,16},{0,24},{9,1},{17,9},{25,17},{1,25},{10,2},{18... | collective-permute-start | bytes 196616 | tf_op jit(solution)/shard_map/ppermute | solution.py:23
  87.4 3.5 %collective-permute-start.21 = (f32[16,4,128]{2,1,0:T(4,128)S(1)}, f32[16,4,128]{2,1,0:T(4,128)S(1)}, u32[]{:S(2)}, u32[]{:S(2)}) collective-permute-start(f32[16,4,128]{2,1,0:T(4,128)S(1)} %get-tuple-element.35), channel_id=1, source_target_pairs={{0,4},{1,5},{2,6},{3,7},{8,12},{9,13},{10,14},{11,15},{16,20},{17,... | collective-permute-start | bytes 98312 | tf_op jit(solution)/shard_map/ppermute | solution.py:20
  89.3 5.8 %collective-permute-start.20 = (f32[16,4,128]{2,1,0:T(4,128)S(1)}, f32[16,4,128]{2,1,0:T(4,128)S(1)}, u32[]{:S(2)}, u32[]{:S(2)}) collective-permute-start(f32[16,4,128]{2,1,0:T(4,128)S(1)} %get-tuple-element.34), channel_id=1, source_target_pairs={{4,0},{5,1},{6,2},{7,3},{12,8},{13,9},{14,10},{15,11},{20,16},{21,... | collective-permute-start | bytes 98312 | tf_op jit(solution)/shard_map/ppermute | solution.py:23
  95.3 9.5 %collective-permute-start.22 = (f32[16,40,4]{2,1,0:T(8,128)S(1)}, f32[16,40,4]{2,1,0:T(8,128)S(1)}, u32[]{:S(2)}, u32[]{:S(2)}) collective-permute-start(f32[16,40,4]{2,1,0:T(8,128)S(1)} %get-tuple-element.12), channel_id=1, source_target_pairs={{1,0},{2,1},{3,2},{5,4},{6,5},{7,6},{9,8},{10,9},{11,10},{13,12},{... | collective-permute-start | bytes 30728 | tf_op jit(solution)/shard_map/ppermute | solution.py:23
  96.6 9.6 %collective-permute-start.23 = (f32[16,40,4]{2,1,0:T(8,128)S(1)}, f32[16,40,4]{2,1,0:T(8,128)S(1)}, u32[]{:S(2)}, u32[]{:S(2)}) collective-permute-start(f32[16,40,4]{2,1,0:T(8,128)S(1)} %get-tuple-element.13), channel_id=1, source_target_pairs={{0,1},{1,2},{2,3},{4,5},{5,6},{6,7},{8,9},{9,10},{10,11},{12,13},{... | collective-permute-start | bytes 30728 | tf_op jit(solution)/shard_map/ppermute | solution.py:20
  101.7 4.9 %collective-permute-start.19 = (f32[4,32,128]{2,1,0:T(8,128)S(1)}, f32[4,32,128]{2,1,0:T(8,128)S(1)}, u32[]{:S(2)}, u32[]{:S(2)}) collective-permute-start(f32[4,32,128]{2,1,0:T(8,128)S(1)} %bitcast.81), channel_id=1, source_target_pairs={{0,8},{8,16},{16,24},{24,0},{1,9},{9,17},{17,25},{25,1},{2,10},{10... | collective-permute-start | bytes 196616 | tf_op jit(solution)/shard_map/ppermute | solution.py:20
  101.8 4.8 %collective-permute-start.18 = (f32[4,32,128]{2,1,0:T(8,128)S(1)}, f32[4,32,128]{2,1,0:T(8,128)S(1)}, u32[]{:S(2)}, u32[]{:S(2)}) collective-permute-start(f32[4,32,128]{2,1,0:T(8,128)S(1)} %bitcast.76), channel_id=1, source_target_pairs={{8,0},{16,8},{24,16},{0,24},{9,1},{17,9},{25,17},{1,25},{10,2},{18... | collective-permute-start | bytes 196616 | tf_op jit(solution)/shard_map/ppermute | solution.py:23
  113.3 3.3 %collective-permute-start.27 = (f32[16,4,128]{2,1,0:T(4,128)S(1)}, f32[16,4,128]{2,1,0:T(4,128)S(1)}, u32[]{:S(2)}, u32[]{:S(2)}) collective-permute-start(f32[16,4,128]{2,1,0:T(4,128)S(1)} %get-tuple-element.31), channel_id=1, source_target_pairs={{0,4},{1,5},{2,6},{3,7},{8,12},{9,13},{10,14},{11,15},{16,20},{17,... | collective-permute-start | bytes 98312 | tf_op jit(solution)/shard_map/ppermute | solution.py:20
  115.0 5.8 %collective-permute-start.26 = (f32[16,4,128]{2,1,0:T(4,128)S(1)}, f32[16,4,128]{2,1,0:T(4,128)S(1)}, u32[]{:S(2)}, u32[]{:S(2)}) collective-permute-start(f32[16,4,128]{2,1,0:T(4,128)S(1)} %get-tuple-element.30), channel_id=1, source_target_pairs={{4,0},{5,1},{6,2},{7,3},{12,8},{13,9},{14,10},{15,11},{20,16},{21,... | collective-permute-start | bytes 98312 | tf_op jit(solution)/shard_map/ppermute | solution.py:23
  121.0 10.6 %collective-permute-start.28 = (f32[16,40,4]{2,1,0:T(8,128)S(1)}, f32[16,40,4]{2,1,0:T(8,128)S(1)}, u32[]{:S(2)}, u32[]{:S(2)}) collective-permute-start(f32[16,40,4]{2,1,0:T(8,128)S(1)} %get-tuple-element.8), channel_id=1, source_target_pairs={{1,0},{2,1},{3,2},{5,4},{6,5},{7,6},{9,8},{10,9},{11,10},{13,12},{... | collective-permute-start | bytes 30728 | tf_op jit(solution)/shard_map/ppermute | solution.py:23
  122.3 10.5 %collective-permute-start.29 = (f32[16,40,4]{2,1,0:T(8,128)S(1)}, f32[16,40,4]{2,1,0:T(8,128)S(1)}, u32[]{:S(2)}, u32[]{:S(2)}) collective-permute-start(f32[16,40,4]{2,1,0:T(8,128)S(1)} %get-tuple-element.9), channel_id=1, source_target_pairs={{0,1},{1,2},{2,3},{4,5},{5,6},{6,7},{8,9},{9,10},{10,11},{12,13},{... | collective-permute-start | bytes 30728 | tf_op jit(solution)/shard_map/ppermute | solution.py:20
  127.4 5.7 %collective-permute-start.25 = (f32[4,32,128]{2,1,0:T(8,128)S(1)}, f32[4,32,128]{2,1,0:T(8,128)S(1)}, u32[]{:S(2)}, u32[]{:S(2)}) collective-permute-start(f32[4,32,128]{2,1,0:T(8,128)S(1)} %bitcast.82), channel_id=1, source_target_pairs={{0,8},{8,16},{16,24},{24,0},{1,9},{9,17},{17,25},{25,1},{2,10},{10... | collective-permute-start | bytes 196616 | tf_op jit(solution)/shard_map/ppermute | solution.py:20
  127.5 5.7 %collective-permute-start.24 = (f32[4,32,128]{2,1,0:T(8,128)S(1)}, f32[4,32,128]{2,1,0:T(8,128)S(1)}, u32[]{:S(2)}, u32[]{:S(2)}) collective-permute-start(f32[4,32,128]{2,1,0:T(8,128)S(1)} %bitcast.77), channel_id=1, source_target_pairs={{8,0},{16,8},{24,16},{0,24},{9,1},{17,9},{25,17},{1,25},{10,2},{18... | collective-permute-start | bytes 196616 | tf_op jit(solution)/shard_map/ppermute | solution.py:23
  139.9 19.5 %copy-start = (f32[65536]{0:T(1024)}, f32[65536]{0:T(1024)S(1)}, u32[]{:S(2)}) copy-start(f32[65536]{0:T(1024)S(1)} %scatter_fusion.4) | copy-start | bytes 786436
  140.0 3.5 %collective-permute-start.33 = (f32[16,4,128]{2,1,0:T(4,128)S(1)}, f32[16,4,128]{2,1,0:T(4,128)S(1)}, u32[]{:S(2)}, u32[]{:S(2)}) collective-permute-start(f32[16,4,128]{2,1,0:T(4,128)S(1)} %get-tuple-element.27), channel_id=1, source_target_pairs={{0,4},{1,5},{2,6},{3,7},{8,12},{9,13},{10,14},{11,15},{16,20},{17,... | collective-permute-start | bytes 98312 | tf_op jit(solution)/shard_map/ppermute | solution.py:20
  141.9 5.8 %collective-permute-start.32 = (f32[16,4,128]{2,1,0:T(4,128)S(1)}, f32[16,4,128]{2,1,0:T(4,128)S(1)}, u32[]{:S(2)}, u32[]{:S(2)}) collective-permute-start(f32[16,4,128]{2,1,0:T(4,128)S(1)} %get-tuple-element.26), channel_id=1, source_target_pairs={{4,0},{5,1},{6,2},{7,3},{12,8},{13,9},{14,10},{15,11},{20,16},{21,... | collective-permute-start | bytes 98312 | tf_op jit(solution)/shard_map/ppermute | solution.py:23
  147.9 10.1 %collective-permute-start.34 = (f32[16,40,4]{2,1,0:T(8,128)S(1)}, f32[16,40,4]{2,1,0:T(8,128)S(1)}, u32[]{:S(2)}, u32[]{:S(2)}) collective-permute-start(f32[16,40,4]{2,1,0:T(8,128)S(1)} %get-tuple-element.4), channel_id=1, source_target_pairs={{1,0},{2,1},{3,2},{5,4},{6,5},{7,6},{9,8},{10,9},{11,10},{13,12},{... | collective-permute-start | bytes 30728 | tf_op jit(solution)/shard_map/ppermute | solution.py:23
  149.2 9.9 %collective-permute-start.35 = (f32[16,40,4]{2,1,0:T(8,128)S(1)}, f32[16,40,4]{2,1,0:T(8,128)S(1)}, u32[]{:S(2)}, u32[]{:S(2)}) collective-permute-start(f32[16,40,4]{2,1,0:T(8,128)S(1)} %get-tuple-element.5), channel_id=1, source_target_pairs={{0,1},{1,2},{2,3},{4,5},{5,6},{6,7},{8,9},{9,10},{10,11},{12,13},{... | collective-permute-start | bytes 30728 | tf_op jit(solution)/shard_map/ppermute | solution.py:20
  154.3 5.2 %collective-permute-start.31 = (f32[4,32,128]{2,1,0:T(8,128)S(1)}, f32[4,32,128]{2,1,0:T(8,128)S(1)}, u32[]{:S(2)}, u32[]{:S(2)}) collective-permute-start(f32[4,32,128]{2,1,0:T(8,128)S(1)} %bitcast.83), channel_id=1, source_target_pairs={{0,8},{8,16},{16,24},{24,0},{1,9},{9,17},{17,25},{25,1},{2,10},{10... | collective-permute-start | bytes 196616 | tf_op jit(solution)/shard_map/ppermute | solution.py:20
  154.3 5.1 %collective-permute-start.30 = (f32[4,32,128]{2,1,0:T(8,128)S(1)}, f32[4,32,128]{2,1,0:T(8,128)S(1)}, u32[]{:S(2)}, u32[]{:S(2)}) collective-permute-start(f32[4,32,128]{2,1,0:T(8,128)S(1)} %bitcast.78), channel_id=1, source_target_pairs={{8,0},{16,8},{24,16},{0,24},{9,1},{17,9},{25,17},{1,25},{10,2},{18... | collective-permute-start | bytes 196616 | tf_op jit(solution)/shard_map/ppermute | solution.py:23
  166.2 0.7 copy-start.3
where the time goes:
time: 168 us; the launch traced here: 167 us
  starting transfers between devices  72.7 us (43%)
  waiting for transfers between devices  43.8 us (26%)
  other arithmetic  42.6 us (25%)
  local copies, waits for them, and re-layouts  6.62 us (4%)
    ppermute x18, starting transfers between devices, padded(): lax.ppermute(lax.slice_in_dim(block, block.shape[dim] - width, None, axis...  46.8 us
    add x6, other arithmetic, per_device(): following = 2.0 * current - before + rate * laplace  35.7 us
    ppermute x18, waiting for transfers between devices, padded(): lax.ppermute(lax.slice_in_dim(block, 0, width, axis=dim), axis, backward)  34.9 us
    ppermute x18, starting transfers between devices, padded(): lax.ppermute(lax.slice_in_dim(block, 0, width, axis=dim), axis, backward)  25.9 us
    ppermute x18, waiting for transfers between devices, padded(): lax.ppermute(lax.slice_in_dim(block, block.shape[dim] - width, None, axis...  8.86 us
    scatter-add x6, other arithmetic, per_device(): following.reshape(-1).at[flat].add(wavelet[step], mode='drop').reshape(size)  4.78 us
  transfers between devices with their start and end apart: 36, of which 23 were waited for; matrix products, arithmetic and copies ran while one was open for 2% of the time, Pallas kernels for 0%

commit v1 on v0

v1 whole, which is shorter than its diff:
```python
import functools

import jax
import jax.numpy as jnp
from jax import lax
from jax.experimental import pallas as pl
from jax.experimental.pallas import tpu as pltpu
from jax.sharding import PartitionSpec as P

STEPS = 6
CENTRE = -205.0 / 72.0
C1, C2, C3, C4 = (8.0 / 5.0, -1.0 / 5.0, 8.0 / 315.0, -1.0 / 560.0)
WEIGHTS = (C1, C2, C3, C4)
W = 4
T = 8
LANES = 128
MESH = pl.DeviceIdType.MESH


def kernel(sizes, now_hbm, before_hbm, code_hbm, vel_ref, wave_ref, src_ref,
           out_hbm, prev_hbm, field, rate, code, source, pack, edge, send_sem, recv_sem, load_sem, store_sem):
    (nx, ny, nz), (gx, gy, gz) = sizes
    grid_y, grid_z = ny * gy, nz * gz
    ix, iy, iz = lax.axis_index("gx"), lax.axis_index("gy"), lax.axis_index("gz")
    x_low, x_high = lax.rem(ix + gx - 1, gx), lax.rem(ix + 1, gx)
    targets = (
        ({"gx": x_low}, None),
        ({"gx": x_high}, None),
        ({"gy": iy - 1}, iy > 0),
        ({"gy": iy + 1}, iy < gy - 1),
        ({"gz": iz - 1}, iz > 0),
        ({"gz": iz + 1}, iz < gz - 1),
    )

    def guarded(condition, action):
        if condition is None:
            action()
        else:
            pl.when(condition)(action)

    own_x, own_y = pl.ds(W, nx), pl.ds(T, ny)
    loads = [
        pltpu.make_async_copy(now_hbm, field.at[0, own_x, own_y], load_sem.at[0]),
        pltpu.make_async_copy(before_hbm, field.at[1, own_x, own_y], load_sem.at[1]),
        pltpu.make_async_copy(code_hbm, code, load_sem.at[2]),
    ]
    for load in loads:
        load.start()

    nothing = jnp.zeros((nx, T, LANES), jnp.float32)
    for par in range(2):
        field[par, own_x, 0:T, :] = nothing
        field[par, own_x, pl.ds(T + ny, T), :] = nothing
    edge[...] = jnp.zeros_like(edge)

    barrier = pltpu.get_barrier_semaphore()
    for target, present in targets:
        guarded(present, lambda target=target: pl.semaphore_signal(
            barrier, inc=1, device_id=target, device_id_type=MESH))

    def copies(par):
        pairs = (
            (field.at[par, pl.ds(W, W), own_y], field.at[par, pl.ds(W + nx, W), own_y]),
            (field.at[par, pl.ds(nx, W), own_y], field.at[par, pl.ds(0, W), own_y]),
            (field.at[par, own_x, pl.ds(T, T)], field.at[par, own_x, pl.ds(T + ny, T)]),
            (field.at[par, own_x, pl.ds(ny, T)], field.at[par, own_x, pl.ds(0, T)]),
            (pack.at[par], edge.at[par, 1]),
            (pack.at[par], edge.at[par, 0]),
        )
        return [
            pltpu.make_async_remote_copy(
                src_ref=src, dst_ref=dst, send_sem=send_sem.at[par, n], recv_sem=recv_sem.at[par, n],
                device_id=target, device_id_type=MESH)
            for n, ((src, dst), (target, _)) in enumerate(zip(pairs, targets))
        ]

    def start(par):
        for copy, (_, present) in zip(copies(par), targets):
            guarded(present, copy.start)

    def wait_send(par):
        for copy, (_, present) in zip(copies(par), targets):
            guarded(present, copy.wait_send)

    def wait_recv(par):
        opposite = (1, 0, 3, 2, 5, 4)
        for n, copy in enumerate(copies(par)):
            guarded(targets[opposite[n]][1], copy.wait_recv)

    lane = lax.broadcasted_iota(jnp.int32, (8, LANES), 1)
    group_of, place = lane // 8, lane % 8
    per_pack = LANES // 8
    slabs = per_pack // 4
    packs = nx // slabs

    def packed(value, g, total):
        return jnp.where(group_of == g, pltpu.roll(value, (W + 8 * g) % LANES, 1), total)

    def rows(j):
        return pl.ds(T + j, 8, stride=4)

    loads[0].wait()

    def first_pack(m, carry):
        total = jnp.zeros((8, LANES), jnp.float32)
        for a in range(slabs):
            for j in range(4):
                total = packed(field[0, W + m * slabs + a, rows(j), :], a * 4 + j, total)
        pack[0, m] = total
        return carry

    lax.fori_loop(0, packs, first_pack, 0)
    peers = 2
    for _, present in targets[2:]:
        peers = peers + present.astype(jnp.int32)
    pl.semaphore_wait(barrier, peers)
    start(0)

    loads[2].wait()
    squares = [vel_ref[n] * vel_ref[n] for n in range(vel_ref.shape[0])]

    def rate_slab(x, carry):
        codes = code[x]
        value = jnp.full(codes.shape, squares[0], jnp.float32)
        for n in range(1, len(squares)):
            value = jnp.where(codes == n, squares[n], value)
        rate[x] = value
        return carry

    lax.fori_loop(0, nx, rate_slab, 0)

    count = src_ref.shape[0]
    row_at = jnp.full((1, LANES), -1, jnp.int32)
    lane_row = lax.broadcasted_iota(jnp.int32, (1, LANES), 1)
    slot_col = lax.broadcasted_iota(jnp.int32, (LANES, LANES), 0)
    z_at = jnp.full((LANES, LANES), -1, jnp.int32)
    for s in range(count):
        cell = src_ref[s]
        sx = cell // (grid_y * grid_z) - ix * nx
        sy = cell // grid_z % grid_y - iy * ny
        sz = cell % grid_z - iz * nz
        here = (sx >= 0) & (sx < nx) & (sy >= 0) & (sy < ny)
        local = jnp.where(here, sx * ny + sy, -1)
        row_at = jnp.where((lane_row % count == s) & (lane_row < 3 * count), local, row_at)
        z_at = jnp.where((slot_col % count == s) & (slot_col < 3 * count), sz, z_at)
    spread = (z_at == lax.broadcasted_iota(jnp.int32, (LANES, LANES), 1)).astype(jnp.float32).astype(jnp.bfloat16)

    def source_field(t):
        wave = jnp.zeros((1, LANES), jnp.float32)
        for s in range(count):
            wave = jnp.where(lane_row % count == s, wave_ref[t, s], wave)
        high = wave.astype(jnp.bfloat16).astype(jnp.float32)
        rest = wave - high
        middle = rest.astype(jnp.bfloat16).astype(jnp.float32)
        parts = jnp.where(lane_row < count, high, jnp.where(lane_row < 2 * count, middle, rest - middle))
        block = slabs * ny

        def chunk(m, carry):
            row = lax.broadcasted_iota(jnp.int32, (block, LANES), 0) + m * block
            picks = jnp.where(row == row_at, parts, 0.0).astype(jnp.bfloat16)
            value = jnp.dot(picks, spread, preferred_element_type=jnp.float32)
            source[pl.ds(m * slabs, slabs)] = value.reshape(slabs, ny, LANES)
            return carry

        lax.fori_loop(0, packs, chunk, 0)

    near_edge = (lane < W) | (lane >= LANES - W)
    take_up = [jnp.where((place >= W) & (place - k < W), WEIGHTS[k - 1], 0.0) for k in range(1, W + 1)]
    take_down = [jnp.where((place < W) & (place + k >= W), WEIGHTS[k - 1], 0.0) for k in range(1, W + 1)]

    loads[1].wait()
    for t in range(STEPS):
        cur, nxt = t % 2, (t + 1) % 2
        source_field(t)
        if t >= 1:
            wait_send(nxt)
        wait_recv(cur)

        def block(m, carry):
            delta = jnp.where(place < W, edge[cur, 0, m], edge[cur, 1, m]) - pack[cur, m]
            fix = jnp.zeros((8, LANES), jnp.float32)
            for k in range(1, W + 1):
                fix = fix + take_up[k - 1] * pltpu.roll(delta, k, 1)
                fix = fix + take_down[k - 1] * pltpu.roll(delta, LANES - k, 1)
            total = jnp.zeros((8, LANES), jnp.float32)
            for a in range(slabs):
                x = m * slabs + a
                shifted = [field[cur, W + x, pl.ds(W + o, 8, stride=4), :] for o in range(12)]
                for j in range(4):
                    g = a * 4 + j
                    f = shifted[4 + j]
                    acc = (3.0 * CENTRE) * f
                    for k in range(1, W + 1):
                        acc = acc + WEIGHTS[k - 1] * (
                            (field[cur, W + x + k, rows(j), :] + field[cur, W + x - k, rows(j), :])
                            + (shifted[4 + j + k] + shifted[4 + j - k]))
                    below, above = pltpu.roll(f, 1, 1), pltpu.roll(f, LANES - 1, 1)
                    far_below = C4 * below + C3 * f + C2 * above
                    far_above = C2 * below + C3 * f + C4 * above
                    acc = acc + C1 * (below + above)
                    acc = acc + pltpu.roll(far_below, 3, 1) + pltpu.roll(far_above, LANES - 3, 1)
                    acc = acc + jnp.where(near_edge, pltpu.roll(fix, (2 * LANES - W - 8 * g) % LANES, 1), 0.0)
                    own = pl.ds(j, 8, stride=4)
                    value = (2.0 * f - field[nxt, W + x, rows(j), :]) + rate[x, own, :] * acc + source[x, own, :]
                    field[nxt, W + x, rows(j), :] = value
                    if t < STEPS - 1:
                        total = packed(value, g, total)
            if t < STEPS - 1:
                pack[nxt, m] = total
            return carry

        lax.fori_loop(0, packs, block, 0)
        if t < STEPS - 1:
            start(nxt)
        if t == STEPS - 2:
            store_prev = pltpu.make_async_copy(field.at[nxt, own_x, own_y], prev_hbm, store_sem.at[0])
            store_prev.start()
    store_out = pltpu.make_async_copy(field.at[STEPS % 2, own_x, own_y], out_hbm, store_sem.at[1])
    store_out.start()
    wait_send((STEPS - 1) % 2)
    store_prev.wait()
    store_out.wait()


def solution(mesh):
    counts = tuple(mesh.shape[name] for name in ("gx", "gy", "gz"))

    def per_device(now, before, codes, velocity, wavelet, source_cell):
        nx, ny, nz = now.shape
        anywhere = pl.BlockSpec(memory_space=pl.ANY)
        scalars = pl.BlockSpec(memory_space=pltpu.SMEM)
        packs = nx * ny // LANES
        return pl.pallas_call(
            functools.partial(kernel, (now.shape, counts)),
            out_shape=(jax.ShapeDtypeStruct(now.shape, jnp.float32),) * 2,
            in_specs=[anywhere] * 3 + [scalars] * 3,
            out_specs=(anywhere, anywhere),
            scratch_shapes=[
                pltpu.VMEM((2, nx + 2 * W, ny + 2 * T, nz), jnp.float32),
                pltpu.VMEM((nx, ny, nz), jnp.float32),
                pltpu.VMEM((nx, ny, nz), jnp.int32),
                pltpu.VMEM((nx, ny, nz), jnp.float32),
                pltpu.VMEM((2, packs, 8, LANES), jnp.float32),
                pltpu.VMEM((2, 2, packs, 8, LANES), jnp.float32),
                pltpu.SemaphoreType.DMA((2, 6)),
                pltpu.SemaphoreType.DMA((2, 6)),
                pltpu.SemaphoreType.DMA((3,)),
                pltpu.SemaphoreType.DMA((2,)),
            ],
            compiler_params=pltpu.CompilerParams(collective_id=0, has_side_effects=True),
        )(now, before, codes, velocity, wavelet, source_cell)

    block = P("gx", "gy", "gz")
    return jax.shard_map(
        per_device,
        mesh=mesh,
        in_specs=(block, block, block, P(), P(), P()),
        out_specs=(block, block),
        check_vma=False,
    )
```

time: 168 us -> 35.4 us (0.21)
  starting transfers between devices: 72.7 us -> 0 us
  waiting for transfers between devices: 43.8 us -> 0 us
  other arithmetic: 42.6 us -> 0 us
  Pallas kernels: 0 us -> 32.1 us
  local copies, waits for them, and re-layouts: 6.62 us -> 2.42 us
    ppermute x36 -> x0, starting transfers between devices: 72.7 us -> none  [the longest x18 46.8 us: padded(): lax.ppermute(lax.slice_in_dim(block, block.shape[dim] - width, None, axis...]
    ppermute x36 -> x0, waiting for transfers between devices: 43.8 us -> none  [the longest x18 34.9 us: padded(): lax.ppermute(lax.slice_in_dim(block, 0, width, axis=dim), axis, backward)]
    add x6 -> x0, other arithmetic: 35.7 us -> none  [per_device(): following = 2.0 * current - before + rate * laplace]
    pallas_call x0 -> x1, Pallas kernels: none -> 32.1 us  [per_device(): pl.pallas_call(functools.partial(kernel, (now.shape, counts)), out_shape=...]
    scatter-add x6 -> x0, other arithmetic: 4.78 us -> none  [per_device(): following.reshape(-1).at[flat].add(wavelet[step], mode='drop').reshape(size)]
    slice x19 -> x0, local copies, waits for them, and re-layouts: 3.57 us -> none  [the longest x18 2.89 us: padded(): lax.slice_in_dim(block, 0, width, axis=dim)]
    concatenate x12 -> x0, other arithmetic: 2.12 us -> none  [padded(): block = jnp.concatenate([low, block, high], axis=dim)]
  transfers between devices with their start and end apart: 36 -> 0, of which waited for: 23 -> 0; matrix products, arithmetic and copies ran while one was open for 2% -> 0% of each run, Pallas kernels for 0% -> 0%
where the time goes in v1:
time: 35.4 us; the launch traced here: 35.2 us
  Pallas kernels  32.1 us (91%)
  local copies, waits for them, and re-layouts  2.42 us (7%)
  between operations  0.65 us (2%)
    pallas_call x1, Pallas kernels, per_device(): pl.pallas_call(functools.partial(kernel, (now.shape, counts)), out_shape=...  32.1 us
    unnamed x4, local copies, waits for them, and re-layouts  2.42 us

profile of v1, /device:TPU:0, one launch (start us, length us, event | category | flops | bytes accessed | tf_op | source)
XLA Modules:
  0.0 35.2 jit_solution(2539186646342603759)
XLA Ops:
  0.6 32.1 %shard_map.77 = (f32[16,32,128]{2,1,0:T(8,128)}, f32[16,32,128]{2,1,0:T(8,128)}) custom-call(f32[16,32,128]{2,1,0:T(8,128)} %now_hbm.1, f32[16,32,128]{2,1,0:T(8,128)} %before_hbm.1, s32[16,32,128]{2,1,0:T(8,128)} %code_hbm.1, f32[8]{0:T(128)} %vel_ref.1, f32[6,16]{1,0:T(8,128)} %wave_ref.1, s32[16]{0:T(128)} %src_ref.1), custom_call_target="tpu_custom_call" | custom-call | tf_op jit(solution)/shard_map/pallas_call | solution.py:233
  32.7 0.0 copy-start
  32.8 1.7 %copy.10 = f32[16,32,128]{2,1,0:T(8,128)} copy(f32[16,32,128]{2,1,0:T(8,128)} %get-tuple-element.4) | data formatting | bytes 524288
  34.5 0.0 copy-done
  34.5 0.7 %copy.11 = f32[16,32,128]{2,1,0:T(8,128)} copy(f32[16,32,128]{2,1,0:T(8,128)S(1)} %copy-done) | data formatting | bytes 524288
Async XLA Ops:
  32.7 1.7 %copy-start = (f32[16,32,128]{2,1,0:T(8,128)S(1)}, f32[16,32,128]{2,1,0:T(8,128)}, u32[]{:S(2)}) copy-start(f32[16,32,128]{2,1,0:T(8,128)} %get-tuple-element.5) | copy-start | bytes 786436

commit v2 on v1

v2 whole, which is shorter than its diff:
```python
import functools

import jax
import jax.numpy as jnp
from jax import lax
from jax.experimental import pallas as pl
from jax.experimental.pallas import tpu as pltpu
from jax.sharding import PartitionSpec as P

STEPS = 6
CENTRE = -205.0 / 72.0
C1, C2, C3, C4 = (8.0 / 5.0, -1.0 / 5.0, 8.0 / 315.0, -1.0 / 560.0)
WEIGHTS = (C1, C2, C3, C4)
W = 4
T = 8
LANES = 128
MESH = pl.DeviceIdType.MESH
def kernel(sizes, now_hbm, before_hbm, code_hbm, vel_ref, wave_ref, src_ref, out_ref, prev_ref,
           field, face, halo, rate, code, source, pack, edge, send_sem, recv_sem, load_sem):
    (nx, ny, nz), (gx, gy, gz) = sizes
    grid_y, grid_z = ny * gy, nz * gz
    lanes_of = ny // 8
    slabs = LANES // 8 // lanes_of
    packs = nx // slabs
    ix, iy, iz = lax.axis_index("gx"), lax.axis_index("gy"), lax.axis_index("gz")
    targets = (
        (({"gx": lax.rem(ix + gx - 1, gx)}, None), ({"gx": lax.rem(ix + 1, gx)}, None)),
        (({"gy": iy - 1}, iy > 0), ({"gy": iy + 1}, iy < gy - 1)),
        (({"gz": iz - 1}, iz > 0), ({"gz": iz + 1}, iz < gz - 1)),
    )

    def guarded(condition, action):
        if condition is None:
            action()
        else:
            pl.when(condition)(action)

    own_x, own_y = pl.ds(0, nx), pl.ds(T, ny)
    loads = [
        pltpu.make_async_copy(now_hbm, field.at[0, own_x, own_y], load_sem.at[0]),
        pltpu.make_async_copy(before_hbm, field.at[1, own_x, own_y], load_sem.at[1]),
        pltpu.make_async_copy(code_hbm, code, load_sem.at[2]),
    ]
    for load in loads:
        load.start()

    nothing = jnp.zeros((nx, T, LANES), jnp.float32)
    for par in range(2):
        field[par, own_x, 0:T, :] = nothing
        field[par, own_x, pl.ds(T + ny, T), :] = nothing
    edge[...] = jnp.zeros_like(edge)

    barrier = pltpu.get_barrier_semaphore()
    for sides in targets:
        for target, present in sides:
            guarded(present, lambda target=target: pl.semaphore_signal(
                barrier, inc=1, device_id=target, device_id_type=MESH))

    inner = packs - 2

    def group(name, par):
        pieces = []
        if name[0] == "x":
            n = name[1]
            base = 2 * n
            pieces = [(0, face.at[par, 0, n], halo.at[par, 1, n]), (0, face.at[par, 1, n], halo.at[par, 0, n])]
        else:
            axis = 1 if name[0] == "y" else 2
            base = 2 * lanes_of + (0 if axis == 1 else 6)
            if axis == 1:
                low, high = pl.ds(T, T), pl.ds(ny, T)
                over, under = pl.ds(T + ny, T), pl.ds(0, T)
                if name[1] == "face":
                    spans = [pl.ds(0, slabs), pl.ds(nx - slabs, slabs)]
                else:
                    spans = [pl.ds(slabs, nx - 2 * slabs)]
                    base = base + 4
                for span in spans:
                    pieces.append((1, field.at[par, span, low], field.at[par, span, over]))
                    pieces.append((1, field.at[par, span, high], field.at[par, span, under]))
            else:
                span = pl.ds(0, 2) if name[1] == "face" else pl.ds(2, inner)
                base = base + (0 if name[1] == "face" else 2)
                pieces.append((2, pack.at[par, span], edge.at[par, 1, span]))
                pieces.append((2, pack.at[par, span], edge.at[par, 0, span]))
        result = []
        for n, (axis, src, dst) in enumerate(pieces):
            target, present = targets[axis][n % 2]
            copy = pltpu.make_async_remote_copy(
                src_ref=src, dst_ref=dst, send_sem=send_sem.at[par, base + n], recv_sem=recv_sem.at[par, base + n],
                device_id=target, device_id_type=MESH)
            result.append((copy, present, targets[axis][1 - n % 2][1]))
        return result

    def start(name, par):
        for copy, to_here, _ in group(name, par):
            guarded(to_here, copy.start)

    def wait_send(name, par):
        for copy, to_here, _ in group(name, par):
            guarded(to_here, copy.wait_send)

    def wait_recv(name, par):
        for copy, _, from_here in group(name, par):
            guarded(from_here, copy.wait_recv)

    chunks = [("x", n) for n in range(lanes_of)]
    every = chunks + [("y", "face"), ("z", "face"), ("y", "inner"), ("z", "inner")]

    lane = lax.broadcasted_iota(jnp.int32, (8, LANES), 1)
    group_of, place = lane // 8, lane % 8

    def packed(value, g, total):
        return jnp.where(group_of == g, pltpu.roll(value, (W + 8 * g) % LANES, 1), total)

    def rows(j):
        return pl.ds(T + j, 8, stride=lanes_of)

    zero = jnp.zeros((8, LANES), jnp.float32)
    ends = ((0, 0, 0), (1, 1, nx - slabs))

    loads[0].wait()
    for side, slot, first in ends:
        total = zero
        for a in range(slabs):
            for j in range(lanes_of):
                value = field[0, first + a, rows(j), :]
                face[0, side, j, a] = value
                total = packed(value, a * lanes_of + j, total)
        pack[0, slot] = total
    peers = 2
    for sides in targets[1:]:
        for _, present in sides:
            peers = peers + present.astype(jnp.int32)
    pl.semaphore_wait(barrier, peers)
    for name in chunks + [("y", "face"), ("z", "face"), ("y", "inner")]:
        start(name, 0)

    def first_pack(m, carry):
        total = zero
        for a in range(slabs):
            for j in range(lanes_of):
                total = packed(field[0, m * slabs + slabs + a, rows(j), :], a * lanes_of + j, total)
        pack[0, 2 + m] = total
        return carry

    lax.fori_loop(0, inner, first_pack, 0)
    start(("z", "inner"), 0)

    loads[2].wait()
    squares = [vel_ref[n] * vel_ref[n] for n in range(vel_ref.shape[0])]

    def rate_slab(x, carry):
        codes = code[x]
        value = jnp.full(codes.shape, squares[0], jnp.float32)
        for n in range(1, len(squares)):
            value = jnp.where(codes == n, squares[n], value)
        rate[x] = value
        return carry

    lax.fori_loop(0, nx, rate_slab, 0)

    count = src_ref.shape[0]
    row_at = jnp.full((1, LANES), -1, jnp.int32)
    lane_row = lax.broadcasted_iota(jnp.int32, (1, LANES), 1)
    slot_col = lax.broadcasted_iota(jnp.int32, (LANES, LANES), 0)
    z_at = jnp.full((LANES, LANES), -1, jnp.int32)
    for s in range(count):
        cell = src_ref[s]
        sx = cell // (grid_y * grid_z) - ix * nx
        sy = cell // grid_z % grid_y - iy * ny
        sz = cell % grid_z - iz * nz
        here = (sx >= 0) & (sx < nx) & (sy >= 0) & (sy < ny)
        local = jnp.where(here, sx * ny + sy, -1)
        row_at = jnp.where((lane_row % count == s) & (lane_row < 3 * count), local, row_at)
        z_at = jnp.where((slot_col % count == s) & (slot_col < 3 * count), sz, z_at)
    spread = (z_at == lax.broadcasted_iota(jnp.int32, (LANES, LANES), 1)).astype(jnp.float32).astype(jnp.bfloat16)

    def source_field(t):
        wave = jnp.zeros((1, LANES), jnp.float32)
        for s in range(count):
            wave = jnp.where(lane_row % count == s, wave_ref[t, s], wave)
        high = wave.astype(jnp.bfloat16).astype(jnp.float32)
        rest = wave - high
        middle = rest.astype(jnp.bfloat16).astype(jnp.float32)
        parts = jnp.where(lane_row < count, high, jnp.where(lane_row < 2 * count, middle, rest - middle))
        block = slabs * ny

        def chunk(m, carry):
            row = lax.broadcasted_iota(jnp.int32, (block, LANES), 0) + m * block
            picks = jnp.where(row == row_at, parts, 0.0).astype(jnp.bfloat16)
            value = jnp.dot(picks, spread, preferred_element_type=jnp.float32)
            source[pl.ds(m * slabs, slabs)] = value.reshape(slabs, ny, LANES)
            return carry

        lax.fori_loop(0, packs, chunk, 0)

    near_edge = (lane < W) | (lane >= LANES - W)
    take_up = [jnp.where((place >= W) & (place - k < W), WEIGHTS[k - 1], 0.0) for k in range(1, W + 1)]
    take_down = [jnp.where((place < W) & (place + k >= W), WEIGHTS[k - 1], 0.0) for k in range(1, W + 1)]

    def edge_fix(cur, slot):
        delta = jnp.where(place < W, edge[cur, 0, slot], edge[cur, 1, slot]) - pack[cur, slot]
        fix = zero
        for k in range(1, W + 1):
            fix = fix + take_up[k - 1] * pltpu.roll(delta, k, 1)
            fix = fix + take_down[k - 1] * pltpu.roll(delta, LANES - k, 1)
        return fix

    def cell_row(cur, nxt, x, a, j, fix, layer):
        def shifted(k):
            return field[cur, x, pl.ds(T + j + k, 8, stride=lanes_of), :]

        f = shifted(0)
        acc = (3.0 * CENTRE) * f
        for k in range(1, W + 1):
            acc = acc + WEIGHTS[k - 1] * ((layer(k) + layer(-k)) + (shifted(k) + shifted(-k)))
        below, above = pltpu.roll(f, 1, 1), pltpu.roll(f, LANES - 1, 1)
        far_below = C4 * below + C3 * f + C2 * above
        far_above = C2 * below + C3 * f + C4 * above
        acc = acc + C1 * (below + above)
        acc = acc + pltpu.roll(far_below, 3, 1) + pltpu.roll(far_above, LANES - 3, 1)
        back = (2 * LANES - W - 8 * (a * lanes_of + j)) % LANES
        acc = acc + jnp.where(near_edge, pltpu.roll(fix, back, 1), 0.0)
        own = pl.ds(j, 8, stride=lanes_of)
        return (2.0 * f - field[nxt, x, rows(j), :]) + rate[x, own, :] * acc + source[x, own, :]

    loads[1].wait()
    for t in range(STEPS):
        cur, nxt = t % 2, (t + 1) % 2
        last = t == STEPS - 1

        def put(x, j, value):
            own = pl.ds(j, 8, stride=lanes_of)
            if last:
                out_ref[x, own, :] = value
            else:
                field[nxt, x, rows(j), :] = value
            if t == STEPS - 2:
                prev_ref[x, own, :] = value

        source_field(t)
        if t >= 1:
            for name in every:
                wait_send(name, nxt)
        wait_recv(("z", "face"), cur)
        wait_recv(("y", "face"), cur)
        fixes = [edge_fix(cur, slot) for _, slot, _ in ends]
        totals = [zero, zero]
        for j in range(lanes_of):
            wait_recv(("x", j), cur)
            for side, slot, first in ends:
                for a in range(slabs):
                    x = first + a

                    def layer(k, x=x, j=j):
                        if x + k < 0:
                            return halo[cur, 0, j, x + k + W]
                        if x + k >= nx:
                            return halo[cur, 1, j, x + k - nx]
                        return field[cur, x + k, rows(j), :]

                    value = cell_row(cur, nxt, x, a, j, fixes[slot], layer)
                    put(x, j, value)
                    if not last:
                        face[nxt, side, j, a] = value
                        totals[slot] = packed(value, a * lanes_of + j, totals[slot])
            if not last:
                start(("x", j), nxt)
        if not last:
            for _, slot, _ in ends:
                pack[nxt, slot] = totals[slot]
            start(("z", "face"), nxt)
            start(("y", "face"), nxt)
        wait_recv(("z", "inner"), cur)
        wait_recv(("y", "inner"), cur)

        def block(m, carry):
            fix = edge_fix(cur, 2 + m)
            total = zero
            for a in range(slabs):
                x = m * slabs + slabs + a
                for j in range(lanes_of):
                    value = cell_row(cur, nxt, x, a, j, fix, lambda k: field[cur, x + k, rows(j), :])
                    put(x, j, value)
                    if not last:
                        total = packed(value, a * lanes_of + j, total)
            if not last:
                pack[nxt, 2 + m] = total
            return carry

        lax.fori_loop(0, inner, block, 0)
        if not last:
            start(("z", "inner"), nxt)
            start(("y", "inner"), nxt)
    for name in every:
        wait_send(name, (STEPS - 1) % 2)


def solution(mesh):
    counts = tuple(mesh.shape[name] for name in ("gx", "gy", "gz"))

    def per_device(now, before, codes, velocity, wavelet, source_cell):
        nx, ny, nz = now.shape
        anywhere = pl.BlockSpec(memory_space=pl.ANY)
        scalars = pl.BlockSpec(memory_space=pltpu.SMEM)
        packs = nx * ny // LANES
        copies = 2 * (ny // 8) + 10
        return pl.pallas_call(
            functools.partial(kernel, (now.shape, counts)),
            out_shape=(pltpu.VMEM(now.shape, jnp.float32),) * 2,
            in_specs=[anywhere] * 3 + [scalars] * 3,
            out_specs=(pl.BlockSpec(memory_space=pltpu.VMEM),) * 2,
            scratch_shapes=[
                pltpu.VMEM((2, nx, ny + 2 * T, nz), jnp.float32),
                pltpu.VMEM((2, 2, ny // 8, W, 8, nz), jnp.float32),
                pltpu.VMEM((2, 2, ny // 8, W, 8, nz), jnp.float32),
                pltpu.VMEM((nx, ny, nz), jnp.float32),
                pltpu.VMEM((nx, ny, nz), jnp.int32),
                pltpu.VMEM((nx, ny, nz), jnp.float32),
                pltpu.VMEM((2, packs, 8, LANES), jnp.float32),
                pltpu.VMEM((2, 2, packs, 8, LANES), jnp.float32),
                pltpu.SemaphoreType.DMA((2, copies)),
                pltpu.SemaphoreType.DMA((2, copies)),
                pltpu.SemaphoreType.DMA((3,)),
            ],
            compiler_params=pltpu.CompilerParams(collective_id=0, has_side_effects=True),
        )(now, before, codes, velocity, wavelet, source_cell)

    block = P("gx", "gy", "gz")
    return jax.shard_map(
        per_device,
        mesh=mesh,
        in_specs=(block, block, block, P(), P(), P()),
        out_specs=(block, block),
        check_vma=False,
    )
```

time: 35.4 us -> 32.2 us (0.910)
  Pallas kernels: 32.1 us -> 29.9 us
  local copies, waits for them, and re-layouts: 2.42 us -> 1.41 us
    pallas_call x1, Pallas kernels: 32.1 us -> 29.9 us  [per_device(): pl.pallas_call(functools.partial(kernel, (now.shape, counts)), out_shape=...]
    unnamed x4 -> x2, local copies, waits for them, and re-layouts: 2.42 us -> 1.41 us
where the time goes in v2:
time: 32.2 us; the launch traced here: 32 us
  Pallas kernels  29.9 us (93%)
  local copies, waits for them, and re-layouts  1.41 us (4%)
  between operations  0.64 us (2%)
    pallas_call x1, Pallas kernels, per_device(): pl.pallas_call(functools.partial(kernel, (now.shape, counts)), out_shape=...  29.9 us
    unnamed x2, local copies, waits for them, and re-layouts  1.41 us

profile of v2, /device:TPU:0, one launch (start us, length us, event | category | flops | bytes accessed | tf_op | source)
XLA Modules:
  0.0 32.0 jit_solution(5095567275356880375)
XLA Ops:
  0.6 29.9 %shard_map.77 = (f32[16,32,128]{2,1,0:T(8,128)S(1)}, f32[16,32,128]{2,1,0:T(8,128)S(1)}) custom-call(f32[16,32,128]{2,1,0:T(8,128)} %now_hbm.1, f32[16,32,128]{2,1,0:T(8,128)} %before_hbm.1, s32[16,32,128]{2,1,0:T(8,128)} %code_hbm.1, f32[8]{0:T(128)} %vel_ref.1, f32[6,16]{1,0:T(8,128)} %wave_ref.1, s32[16]{0:T(128)} %src_ref.1), custom_call_target="tpu_custom_call" | custom-call | tf_op jit(solution)/shard_map/pallas_call | solution.py:309
  30.6 0.7 %copy.10 = f32[16,32,128]{2,1,0:T(8,128)} copy(f32[16,32,128]{2,1,0:T(8,128)S(1)} %get-tuple-element.2) | data formatting | bytes 524288
  31.3 0.7 %copy.11 = f32[16,32,128]{2,1,0:T(8,128)} copy(f32[16,32,128]{2,1,0:T(8,128)S(1)} %get-tuple-element.3) | data formatting | bytes 524288

commit v3 on v2

--- a/solution.py
+++ b/solution.py
@@ -12,11 +12,12 @@
 C1, C2, C3, C4 = (8.0 / 5.0, -1.0 / 5.0, 8.0 / 315.0, -1.0 / 560.0)
 WEIGHTS = (C1, C2, C3, C4)
 W = 4
+CHUNKS = 2
 T = 8
 LANES = 128
 MESH = pl.DeviceIdType.MESH
 def kernel(sizes, now_hbm, before_hbm, code_hbm, vel_ref, wave_ref, src_ref, out_ref, prev_ref,
-           field, face, halo, rate, code, source, pack, edge, send_sem, recv_sem, load_sem):
+           field, state, halo, rate, code, source, pack, edge, send_sem, recv_sem, load_sem):
     (nx, ny, nz), (gx, gy, gz) = sizes
     grid_y, grid_z = ny * gy, nz * gz
     lanes_of = ny // 8
@@ -36,6 +37,7 @@
             pl.when(condition)(action)
 
     own_x, own_y = pl.ds(0, nx), pl.ds(T, ny)
+    half = lanes_of // CHUNKS
     loads = [
         pltpu.make_async_copy(now_hbm, field.at[0, own_x, own_y], load_sem.at[0]),
         pltpu.make_async_copy(before_hbm, field.at[1, own_x, own_y], load_sem.at[1]),
@@ -61,12 +63,13 @@
     def group(name, par):
         pieces = []
         if name[0] == "x":
-            n = name[1]
-            base = 2 * n
-            pieces = [(0, face.at[par, 0, n], halo.at[par, 1, n]), (0, face.at[par, 1, n], halo.at[par, 0, n])]
+            base = 2 * name[1]
+            part = pl.ds(name[1] * half, half)
+            pieces = [(0, state.at[par, pl.ds(0, W), part], halo.at[par, 1, name[1]]),
+                      (0, state.at[par, pl.ds(nx - W, W), part], halo.at[par, 0, name[1]])]
         else:
             axis = 1 if name[0] == "y" else 2
-            base = 2 * lanes_of + (0 if axis == 1 else 6)
+            base = 2 * CHUNKS + (0 if axis == 1 else 6)
             if axis == 1:
                 low, high = pl.ds(T, T), pl.ds(ny, T)
                 over, under = pl.ds(T + ny, T), pl.ds(0, T)
@@ -104,7 +107,7 @@
         for copy, _, from_here in group(name, par):
             guarded(from_here, copy.wait_recv)
 
-    chunks = [("x", n) for n in range(lanes_of)]
+    chunks = [("x", n) for n in range(CHUNKS)]
     every = chunks + [("y", "face"), ("z", "face"), ("y", "inner"), ("z", "inner")]
 
     lane = lax.broadcasted_iota(jnp.int32, (8, LANES), 1)
@@ -125,7 +128,7 @@
         for a in range(slabs):
             for j in range(lanes_of):
                 value = field[0, first + a, rows(j), :]
-                face[0, side, j, a] = value
+                state[0, first + a, j] = value
                 total = packed(value, a * lanes_of + j, total)
         pack[0, slot] = total
     peers = 2
@@ -140,7 +143,9 @@
         total = zero
         for a in range(slabs):
             for j in range(lanes_of):
-                total = packed(field[0, m * slabs + slabs + a, rows(j), :], a * lanes_of + j, total)
+                value = field[0, m * slabs + slabs + a, rows(j), :]
+                state[0, m * slabs + slabs + a, j] = value
+                total = packed(value, a * lanes_of + j, total)
         pack[0, 2 + m] = total
         return carry
 
@@ -151,11 +156,12 @@
     squares = [vel_ref[n] * vel_ref[n] for n in range(vel_ref.shape[0])]
 
     def rate_slab(x, carry):
-        codes = code[x]
-        value = jnp.full(codes.shape, squares[0], jnp.float32)
-        for n in range(1, len(squares)):
-            value = jnp.where(codes == n, squares[n], value)
-        rate[x] = value
+        for j in range(lanes_of):
+            codes = code[x, pl.ds(j, 8, stride=lanes_of), :]
+            value = jnp.full(codes.shape, squares[0], jnp.float32)
+            for n in range(1, len(squares)):
+                value = jnp.where(codes == n, squares[n], value)
+            rate[x, j] = value
         return carry
 
     lax.fori_loop(0, nx, rate_slab, 0)
@@ -171,7 +177,7 @@
         sy = cell // grid_z % grid_y - iy * ny
         sz = cell % grid_z - iz * nz
         here = (sx >= 0) & (sx < nx) & (sy >= 0) & (sy < ny)
-        local = jnp.where(here, sx * ny + sy, -1)
+        local = jnp.where(here, sx * ny + sy % lanes_of * 8 + sy // lanes_of, -1)
         row_at = jnp.where((lane_row % count == s) & (lane_row < 3 * count), local, row_at)
         z_at = jnp.where((slot_col % count == s) & (slot_col < 3 * count), sz, z_at)
     spread = (z_at == lax.broadcasted_iota(jnp.int32, (LANES, LANES), 1)).astype(jnp.float32).astype(jnp.bfloat16)
@@ -190,7 +196,7 @@
             row = lax.broadcasted_iota(jnp.int32, (block, LANES), 0) + m * block
             picks = jnp.where(row == row_at, parts, 0.0).astype(jnp.bfloat16)
             value = jnp.dot(picks, spread, preferred_element_type=jnp.float32)
-            source[pl.ds(m * slabs, slabs)] = value.reshape(slabs, ny, LANES)
+            source[pl.ds(m * slabs, slabs)] = value.reshape(slabs, lanes_of, 8, LANES)
             return carry
 
         lax.fori_loop(0, packs, chunk, 0)
@@ -207,25 +213,36 @@
             fix = fix + take_down[k - 1] * pltpu.roll(delta, LANES - k, 1)
         return fix
 
-    def cell_row(cur, nxt, x, a, j, fix, layer):
-        def shifted(k):
-            return field[cur, x, pl.ds(T + j + k, 8, stride=lanes_of), :]
-
-        f = shifted(0)
-        acc = (3.0 * CENTRE) * f
-        for k in range(1, W + 1):
-            acc = acc + WEIGHTS[k - 1] * ((layer(k) + layer(-k)) + (shifted(k) + shifted(-k)))
-        below, above = pltpu.roll(f, 1, 1), pltpu.roll(f, LANES - 1, 1)
-        far_below = C4 * below + C3 * f + C2 * above
-        far_above = C2 * below + C3 * f + C4 * above
-        acc = acc + C1 * (below + above)
-        acc = acc + pltpu.roll(far_below, 3, 1) + pltpu.roll(far_above, LANES - 3, 1)
-        back = (2 * LANES - W - 8 * (a * lanes_of + j)) % LANES
-        acc = acc + jnp.where(near_edge, pltpu.roll(fix, back, 1), 0.0)
-        own = pl.ds(j, 8, stride=lanes_of)
-        return (2.0 * f - field[nxt, x, rows(j), :]) + rate[x, own, :] * acc + source[x, own, :]
+    def cell_rows(cur, nxt, x, a, js, fix, layer):
+        shifted = {}
+        for o in range(js[0] - W, js[-1] + W + 1):
+            if 0 <= o < lanes_of:
+                shifted[o] = state[cur, x, o]
+            else:
+                shifted[o] = field[cur, x, pl.ds(T + o, 8, stride=lanes_of), :]
+        values = []
+        for j in js:
+            f = shifted[j]
+            acc = (3.0 * CENTRE) * f
+            for k in range(1, W + 1):
+                acc = acc + WEIGHTS[k - 1] * ((layer(k, j) + layer(-k, j)) + (shifted[j + k] + shifted[j - k]))
+            below, above = pltpu.roll(f, 1, 1), pltpu.roll(f, LANES - 1, 1)
+            far_below = C4 * below + C3 * f + C2 * above
+            far_above = C2 * below + C3 * f + C4 * above
+            acc = acc + C1 * (below + above)
+            acc = acc + pltpu.roll(far_below, 3, 1) + pltpu.roll(far_above, LANES - 3, 1)
+            back = (2 * LANES - W - 8 * (a * lanes_of + j)) % LANES
+            acc = acc + jnp.where(near_edge, pltpu.roll(fix, back, 1), 0.0)
+            values.append((2.0 * f - state[nxt, x, j]) + rate[x, j] * acc + source[x, j])
+        return values
+
+    def first_before(x, carry):
+        for j in range(lanes_of):
+            state[1, x, j] = field[1, x, rows(j), :]
+        return carry
 
     loads[1].wait()
+    lax.fori_loop(0, nx, first_before, 0)
     for t in range(STEPS):
         cur, nxt = t % 2, (t + 1) % 2
         last = t == STEPS - 1
@@ -235,6 +252,7 @@
             if last:
                 out_ref[x, own, :] = value
             else:
+                state[nxt, x, j] = value
                 field[nxt, x, rows(j), :] = value
             if t == STEPS - 2:
                 prev_ref[x, own, :] = value
@@ -247,26 +265,26 @@
         wait_recv(("y", "face"), cur)
         fixes = [edge_fix(cur, slot) for _, slot, _ in ends]
         totals = [zero, zero]
-        for j in range(lanes_of):
-            wait_recv(("x", j), cur)
+        for n in range(CHUNKS):
+            wait_recv(("x", n), cur)
+            js = range(n * half, n * half + half)
             for side, slot, first in ends:
                 for a in range(slabs):
                     x = first + a
 
-                    def layer(k, x=x, j=j):
+                    def layer(k, j, x=x, n=n):
                         if x + k < 0:
-                            return halo[cur, 0, j, x + k + W]
+                            return halo[cur, 0, n, x + k + W, j - n * half]
                         if x + k >= nx:
-                            return halo[cur, 1, j, x + k - nx]
-                        return field[cur, x + k, rows(j), :]
-
-                    value = cell_row(cur, nxt, x, a, j, fixes[slot], layer)
-                    put(x, j, value)
-                    if not last:
-                        face[nxt, side, j, a] = value
-                        totals[slot] = packed(value, a * lanes_of + j, totals[slot])
+                            return halo[cur, 1, n, x + k - nx, j - n * half]
+                        return state[cur, x + k, j]
+
+                    for j, value in zip(js, cell_rows(cur, nxt, x, a, js, fixes[slot], layer)):
+                        put(x, j, value)
+                        if not last:
+                            totals[slot] = packed(value, a * lanes_of + j, totals[slot])
             if not last:
-                start(("x", j), nxt)
+                start(("x", n), nxt)
         if not last:
             for _, slot, _ in ends:
                 pack[nxt, slot] = totals[slot]
@@ -280,8 +298,9 @@
             total = zero
             for a in range(slabs):
                 x = m * slabs + slabs + a
-                for j in range(lanes_of):
-                    value = cell_row(cur, nxt, x, a, j, fix, lambda k: field[cur, x + k, rows(j), :])
+                js = range(lanes_of)
+                near = lambda k, j: state[cur, x + k, j]
+                for j, value in zip(js, cell_rows(cur, nxt, x, a, js, fix, near)):
                     put(x, j, value)
                     if not last:
                         total = packed(value, a * lanes_of + j, total)
@@ -297,6 +316,17 @@
         wait_send(name, (STEPS - 1) % 2)
 
 
+def move_out(first_ref, second_ref, first_out, second_out, sem):
+    moves = [
+        pltpu.make_async_copy(first_ref, first_out, sem.at[0]),
+        pltpu.make_async_copy(second_ref, second_out, sem.at[1]),
+    ]
+    for move in moves:
+        move.start()
+    for move in moves:
+        move.wait()
+
+
 def solution(mesh):
     counts = tuple(mesh.shape[name] for name in ("gx", "gy", "gz"))
 
@@ -305,19 +335,19 @@
         anywhere = pl.BlockSpec(memory_space=pl.ANY)
         scalars = pl.BlockSpec(memory_space=pltpu.SMEM)
         packs = nx * ny // LANES
-        copies = 2 * (ny // 8) + 10
-        return pl.pallas_call(
+        copies = 2 * CHUNKS + 10
+        results = pl.pallas_call(
             functools.partial(kernel, (now.shape, counts)),
             out_shape=(pltpu.VMEM(now.shape, jnp.float32),) * 2,
             in_specs=[anywhere] * 3 + [scalars] * 3,
             out_specs=(pl.BlockSpec(memory_space=pltpu.VMEM),) * 2,
             scratch_shapes=[
                 pltpu.VMEM((2, nx, ny + 2 * T, nz), jnp.float32),
-                pltpu.VMEM((2, 2, ny // 8, W, 8, nz), jnp.float32),
-                pltpu.VMEM((2, 2, ny // 8, W, 8, nz), jnp.float32),
-                pltpu.VMEM((nx, ny, nz), jnp.float32),
+                pltpu.VMEM((2, nx, ny // 8, 8, nz), jnp.float32),
+                pltpu.VMEM((2, 2, CHUNKS, W, ny // 8 // CHUNKS, 8, nz), jnp.float32),
+                pltpu.VMEM((nx, ny // 8, 8, nz), jnp.float32),
                 pltpu.VMEM((nx, ny, nz), jnp.int32),
-                pltpu.VMEM((nx, ny, nz), jnp.float32),
+                pltpu.VMEM((nx, ny // 8, 8, nz), jnp.float32),
                 pltpu.VMEM((2, packs, 8, LANES), jnp.float32),
                 pltpu.VMEM((2, 2, packs, 8, LANES), jnp.float32),
                 pltpu.SemaphoreType.DMA((2, copies)),
@@ -326,6 +356,14 @@
             ],
             compiler_params=pltpu.CompilerParams(collective_id=0, has_side_effects=True),
         )(now, before, codes, velocity, wavelet, source_cell)
+        return pl.pallas_call(
+            move_out,
+            out_shape=(jax.ShapeDtypeStruct(now.shape, jnp.float32),) * 2,
+            in_specs=[pl.BlockSpec(memory_space=pltpu.VMEM)] * 2,
+            out_specs=(anywhere, anywhere),
+            scratch_shapes=[pltpu.SemaphoreType.DMA((2,))],
+            compiler_params=pltpu.CompilerParams(vmem_limit_bytes=2**20),
+        )(*[pltpu.with_memory_space_constraint(value, pltpu.VMEM) for value in results])
 
     block = P("gx", "gy", "gz")
     return jax.shard_map(

time: 32.2 us -> 29.2 us (0.907)
  Pallas kernels: 29.9 us -> 28.4 us
  local copies, waits for them, and re-layouts: 1.41 us -> 0 us
    pallas_call x1, Pallas kernels: 29.9 us -> 27.6 us  [per_device(): pl.pallas_call(functools.partial(kernel, (now.shape, counts)), out_shape=...]
    unnamed x2 -> x0, local copies, waits for them, and re-layouts: 1.41 us -> none
    pallas_call x0 -> x1, Pallas kernels: none -> 0.81 us  [per_device(): pl.pallas_call(move_out, out_shape=(jax.ShapeDtypeStruct(now.shape, jnp.f...]
where the time goes in v3:
time: 29.2 us; the launch traced here: 29 us
  Pallas kernels  28.4 us (97%)
  between operations  0.64 us (2%)
    pallas_call x1, Pallas kernels, per_device(): pl.pallas_call(functools.partial(kernel, (now.shape, counts)), out_shape=...  27.6 us
    pallas_call x1, Pallas kernels, per_device(): pl.pallas_call(move_out, out_shape=(jax.ShapeDtypeStruct(now.shape, jnp.f...  0.81 us

profile of v3, /device:TPU:0, one launch (start us, length us, event | category | flops | bytes accessed | tf_op | source)
XLA Modules:
  0.0 29.0 jit_solution(2413902604482165548)
XLA Ops:
  0.6 27.6 %shard_map.77 = (f32[16,32,128]{2,1,0:T(8,128)S(1)}, f32[16,32,128]{2,1,0:T(8,128)S(1)}) custom-call(f32[16,32,128]{2,1,0:T(8,128)} %now_hbm.1, f32[16,32,128]{2,1,0:T(8,128)} %before_hbm.1, s32[16,32,128]{2,1,0:T(8,128)} %code_hbm.1, f32[8]{0:T(128)} %vel_ref.1, f32[6,16]{1,0:T(8,128)} %wave_ref.1, s32[16]{0:T(128)} %src_ref.1), custom_call_target="tpu_custom_call" | custom-call | tf_op jit(solution)/shard_map/pallas_call | solution.py:339
  28.2 0.8 %shard_map.78 = (f32[16,32,128]{2,1,0:T(8,128)}, f32[16,32,128]{2,1,0:T(8,128)}) custom-call(f32[16,32,128]{2,1,0:T(8,128)S(1)} %get-tuple-element.4.first_ref, f32[16,32,128]{2,1,0:T(8,128)S(1)} %get-tuple-element.5.second_ref), custom_call_target="tpu_custom_call" | custom-call | tf_op jit(solution)/shard_map/pallas_call | solution.py:359

commit v4 on v3

--- a/solution.py
+++ b/solution.py
@@ -12,12 +12,13 @@
 C1, C2, C3, C4 = (8.0 / 5.0, -1.0 / 5.0, 8.0 / 315.0, -1.0 / 560.0)
 WEIGHTS = (C1, C2, C3, C4)
 W = 4
-CHUNKS = 2
+CHUNKS = 1
 T = 8
 LANES = 128
 MESH = pl.DeviceIdType.MESH
 def kernel(sizes, now_hbm, before_hbm, code_hbm, vel_ref, wave_ref, src_ref, out_ref, prev_ref,
-           field, state, halo, rate, code, source, pack, edge, send_sem, recv_sem, load_sem):
+           field0, field1, state0, state1, pack0, pack1, halo, rate, code, source, edge, send_sem, recv_sem, load_sem):
+    field, state, pack = (field0, field1), (state0, state1), (pack0, pack1)
     (nx, ny, nz), (gx, gy, gz) = sizes
     grid_y, grid_z = ny * gy, nz * gz
     lanes_of = ny // 8
@@ -39,8 +40,8 @@
     own_x, own_y = pl.ds(0, nx), pl.ds(T, ny)
     half = lanes_of // CHUNKS
     loads = [
-        pltpu.make_async_copy(now_hbm, field.at[0, own_x, own_y], load_sem.at[0]),
-        pltpu.make_async_copy(before_hbm, field.at[1, own_x, own_y], load_sem.at[1]),
+        pltpu.make_async_copy(now_hbm, field[0].at[own_x, own_y], load_sem.at[0]),
+        pltpu.make_async_copy(before_hbm, field[1].at[own_x, own_y], load_sem.at[1]),
         pltpu.make_async_copy(code_hbm, code, load_sem.at[2]),
     ]
     for load in loads:
@@ -48,8 +49,8 @@
 
     nothing = jnp.zeros((nx, T, LANES), jnp.float32)
     for par in range(2):
-        field[par, own_x, 0:T, :] = nothing
-        field[par, own_x, pl.ds(T + ny, T), :] = nothing
+        field[par][own_x, 0:T, :] = nothing
+        field[par][own_x, pl.ds(T + ny, T), :] = nothing
     edge[...] = jnp.zeros_like(edge)
 
     barrier = pltpu.get_barrier_semaphore()
@@ -65,8 +66,8 @@
         if name[0] == "x":
             base = 2 * name[1]
             part = pl.ds(name[1] * half, half)
-            pieces = [(0, state.at[par, pl.ds(0, W), part], halo.at[par, 1, name[1]]),
-                      (0, state.at[par, pl.ds(nx - W, W), part], halo.at[par, 0, name[1]])]
+            pieces = [(0, state[par].at[pl.ds(0, W), part], halo.at[par, 1, name[1]]),
+                      (0, state[par].at[pl.ds(nx - W, W), part], halo.at[par, 0, name[1]])]
         else:
             axis = 1 if name[0] == "y" else 2
             base = 2 * CHUNKS + (0 if axis == 1 else 6)
@@ -79,13 +80,13 @@
                     spans = [pl.ds(slabs, nx - 2 * slabs)]
                     base = base + 4
                 for span in spans:
-                    pieces.append((1, field.at[par, span, low], field.at[par, span, over]))
-                    pieces.append((1, field.at[par, span, high], field.at[par, span, under]))
+                    pieces.append((1, field[par].at[span, low], field[par].at[span, over]))
+                    pieces.append((1, field[par].at[span, high], field[par].at[span, under]))
             else:
                 span = pl.ds(0, 2) if name[1] == "face" else pl.ds(2, inner)
                 base = base + (0 if name[1] == "face" else 2)
-                pieces.append((2, pack.at[par, span], edge.at[par, 1, span]))
-                pieces.append((2, pack.at[par, span], edge.at[par, 0, span]))
+                pieces.append((2, pack[par].at[span], edge.at[par, 1, span]))
+                pieces.append((2, pack[par].at[span], edge.at[par, 0, span]))
         result = []
         for n, (axis, src, dst) in enumerate(pieces):
             target, present = targets[axis][n % 2]
@@ -127,10 +128,10 @@
         total = zero
         for a in range(slabs):
             for j in range(lanes_of):
-                value = field[0, first + a, rows(j), :]
-                state[0, first + a, j] = value
+                value = field[0][first + a, rows(j), :]
+                state[0][first + a, j] = value
                 total = packed(value, a * lanes_of + j, total)
-        pack[0, slot] = total
+        pack[0][slot] = total
     peers = 2
     for sides in targets[1:]:
         for _, present in sides:
@@ -143,10 +144,10 @@
         total = zero
         for a in range(slabs):
             for j in range(lanes_of):
-                value = field[0, m * slabs + slabs + a, rows(j), :]
-                state[0, m * slabs + slabs + a, j] = value
+                value = field[0][m * slabs + slabs + a, rows(j), :]
+                state[0][m * slabs + slabs + a, j] = value
                 total = packed(value, a * lanes_of + j, total)
-        pack[0, 2 + m] = total
+        pack[0][2 + m] = total
         return carry
 
     lax.fori_loop(0, inner, first_pack, 0)
@@ -206,7 +207,7 @@
     take_down = [jnp.where((place < W) & (place + k >= W), WEIGHTS[k - 1], 0.0) for k in range(1, W + 1)]
 
     def edge_fix(cur, slot):
-        delta = jnp.where(place < W, edge[cur, 0, slot], edge[cur, 1, slot]) - pack[cur, slot]
+        delta = jnp.where(place < W, edge[cur, 0, slot], edge[cur, 1, slot]) - pack[cur][slot]
         fix = zero
         for k in range(1, W + 1):
             fix = fix + take_up[k - 1] * pltpu.roll(delta, k, 1)
@@ -217,9 +218,9 @@
         shifted = {}
         for o in range(js[0] - W, js[-1] + W + 1):
             if 0 <= o < lanes_of:
-                shifted[o] = state[cur, x, o]
+                shifted[o] = state[cur][x, o]
             else:
-                shifted[o] = field[cur, x, pl.ds(T + o, 8, stride=lanes_of), :]
+                shifted[o] = field[cur][x, pl.ds(T + o, 8, stride=lanes_of), :]
         values = []
         for j in js:
             f = shifted[j]
@@ -233,12 +234,12 @@
             acc = acc + pltpu.roll(far_below, 3, 1) + pltpu.roll(far_above, LANES - 3, 1)
             back = (2 * LANES - W - 8 * (a * lanes_of + j)) % LANES
             acc = acc + jnp.where(near_edge, pltpu.roll(fix, back, 1), 0.0)
-            values.append((2.0 * f - state[nxt, x, j]) + rate[x, j] * acc + source[x, j])
+            values.append((2.0 * f - state[nxt][x, j]) + rate[x, j] * acc + source[x, j])
         return values
 
     def first_before(x, carry):
         for j in range(lanes_of):
-            state[1, x, j] = field[1, x, rows(j), :]
+            state[1][x, j] = field[1][x, rows(j), :]
         return carry
 
     loads[1].wait()
@@ -252,8 +253,8 @@
             if last:
                 out_ref[x, own, :] = value
             else:
-                state[nxt, x, j] = value
-                field[nxt, x, rows(j), :] = value
+                state[nxt][x, j] = value
+                field[nxt][x, rows(j), :] = value
             if t == STEPS - 2:
                 prev_ref[x, own, :] = value
 
@@ -277,7 +278,7 @@
                             return halo[cur, 0, n, x + k + W, j - n * half]
                         if x + k >= nx:
                             return halo[cur, 1, n, x + k - nx, j - n * half]
-                        return state[cur, x + k, j]
+                        return state[cur][x + k, j]
 
                     for j, value in zip(js, cell_rows(cur, nxt, x, a, js, fixes[slot], layer)):
                         put(x, j, value)
@@ -287,7 +288,7 @@
                 start(("x", n), nxt)
         if not last:
             for _, slot, _ in ends:
-                pack[nxt, slot] = totals[slot]
+                pack[nxt][slot] = totals[slot]
             start(("z", "face"), nxt)
             start(("y", "face"), nxt)
         wait_recv(("z", "inner"), cur)
@@ -299,13 +300,13 @@
             for a in range(slabs):
                 x = m * slabs + slabs + a
                 js = range(lanes_of)
-                near = lambda k, j: state[cur, x + k, j]
+                near = lambda k, j: state[cur][x + k, j]
                 for j, value in zip(js, cell_rows(cur, nxt, x, a, js, fix, near)):
                     put(x, j, value)
                     if not last:
                         total = packed(value, a * lanes_of + j, total)
             if not last:
-                pack[nxt, 2 + m] = total
+                pack[nxt][2 + m] = total
             return carry
 
         lax.fori_loop(0, inner, block, 0)
@@ -342,13 +343,16 @@
             in_specs=[anywhere] * 3 + [scalars] * 3,
             out_specs=(pl.BlockSpec(memory_space=pltpu.VMEM),) * 2,
             scratch_shapes=[
-                pltpu.VMEM((2, nx, ny + 2 * T, nz), jnp.float32),
-                pltpu.VMEM((2, nx, ny // 8, 8, nz), jnp.float32),
+                pltpu.VMEM((nx, ny + 2 * T, nz), jnp.float32),
+                pltpu.VMEM((nx, ny + 2 * T, nz), jnp.float32),
+                pltpu.VMEM((nx, ny // 8, 8, nz), jnp.float32),
+                pltpu.VMEM((nx, ny // 8, 8, nz), jnp.float32),
+                pltpu.VMEM((packs, 8, LANES), jnp.float32),
+                pltpu.VMEM((packs, 8, LANES), jnp.float32),
                 pltpu.VMEM((2, 2, CHUNKS, W, ny // 8 // CHUNKS, 8, nz), jnp.float32),
                 pltpu.VMEM((nx, ny // 8, 8, nz), jnp.float32),
                 pltpu.VMEM((nx, ny, nz), jnp.int32),
                 pltpu.VMEM((nx, ny // 8, 8, nz), jnp.float32),
-                pltpu.VMEM((2, packs, 8, LANES), jnp.float32),
                 pltpu.VMEM((2, 2, packs, 8, LANES), jnp.float32),
                 pltpu.SemaphoreType.DMA((2, copies)),
                 pltpu.SemaphoreType.DMA((2, copies)),

time: 29.2 us -> 28.9 us (0.990)
  Pallas kernels: 28.4 us -> 28 us
    pallas_call x1, Pallas kernels: 27.6 us -> 27.2 us  [per_device(): pl.pallas_call(functools.partial(kernel, (now.shape, counts)), out_shape=...]
where the time goes in v4:
time: 28.9 us; the launch traced here: 28.7 us
  Pallas kernels  28 us (97%)
  between operations  0.64 us (2%)
    pallas_call x1, Pallas kernels, per_device(): pl.pallas_call(functools.partial(kernel, (now.shape, counts)), out_shape=...  27.2 us
    pallas_call x1, Pallas kernels, per_device(): pl.pallas_call(move_out, out_shape=(jax.ShapeDtypeStruct(now.shape, jnp.f...  0.81 us

profile of v4, /device:TPU:0, one launch (start us, length us, event | category | flops | bytes accessed | tf_op | source)
XLA Modules:
  0.0 28.7 jit_solution(14627282900959597855)
XLA Ops:
  0.6 27.2 %shard_map.77 = (f32[16,32,128]{2,1,0:T(8,128)S(1)}, f32[16,32,128]{2,1,0:T(8,128)S(1)}) custom-call(f32[16,32,128]{2,1,0:T(8,128)} %now_hbm.1, f32[16,32,128]{2,1,0:T(8,128)} %before_hbm.1, s32[16,32,128]{2,1,0:T(8,128)} %code_hbm.1, f32[8]{0:T(128)} %vel_ref.1, f32[6,16]{1,0:T(8,128)} %wave_ref.1, s32[16]{0:T(128)} %src_ref.1), custom_call_target="tpu_custom_call" | custom-call | tf_op jit(solution)/shard_map/pallas_call | solution.py:340
  27.9 0.8 %shard_map.78 = (f32[16,32,128]{2,1,0:T(8,128)}, f32[16,32,128]{2,1,0:T(8,128)}) custom-call(f32[16,32,128]{2,1,0:T(8,128)S(1)} %get-tuple-element.4.first_ref, f32[16,32,128]{2,1,0:T(8,128)S(1)} %get-tuple-element.5.second_ref), custom_call_target="tpu_custom_call" | custom-call | tf_op jit(solution)/shard_map/pallas_call | solution.py:363
